TPU v7x, 32 devices: a whole 2x2x4 slice. The times are simulated.
32 devices in a mesh: dp: 4 (over y, core), fsdp: 2 (over x), seq: 4 (over z).
Axes of the slice: x: 2, y: 2, z: 4, core: 2. Of those that a mesh axis runs over, the one named last changes fastest.
Arguments:
- frames_in: float32 [8, 1536, 768], P(('dp', 'fsdp'), 'seq'), may hold values from -8 to 8
- cotangent: float32 [8, 1536, 768], P(('dp', 'fsdp'), 'seq'), may hold values from -6 to 6
- attention_weight: float32 [4, 768, 768], P(None, 'fsdp'), may hold values from -16 to 16
- expand_weight: float32 [768, 3072], P('fsdp'), may hold values from -0.21875 to 0.21875
- contract_weight: float32 [3072, 768], P('fsdp'), may hold values from -0.109375 to 0.109375
- vectors: float32 [12, 768], P(None, 'fsdp'), may hold values from -2 to 2
- first_attention: float32 [4, 768, 768], P(None, 'fsdp'), may hold values from -32 to 32
- first_expand: float32 [768, 3072], P('fsdp'), may hold values from -32 to 32
- first_contract: float32 [3072, 768], P('fsdp'), may hold values from -32 to 32
- first_vectors: float32 [12, 768], P(None, 'fsdp'), may hold values from -32 to 32
- second_attention: float32 [4, 768, 768], P(None, 'fsdp'), may hold values from 0.24576 to 4.9152
- second_expand: float32 [768, 3072], P('fsdp'), may hold values from 0.24576 to 4.9152
- second_contract: float32 [3072, 768], P('fsdp'), may hold values from 0.24576 to 4.9152
- second_vectors: float32 [12, 768], P(None, 'fsdp'), may hold values from 0.24576 to 4.9152
Outputs:
- frames_out: float32 [8, 1536, 768], P(('dp', 'fsdp'), 'seq')
- input_gradient: float32 [8, 1536, 768], P(('dp', 'fsdp'), 'seq')
- gradient_attention: float32 [4, 768, 768], P(None, 'fsdp')
- gradient_expand: float32 [768, 3072], P('fsdp')
- gradient_contract: float32 [3072, 768], P('fsdp')
- gradient_vectors: float32 [12, 768], P(None, 'fsdp')
- updated_attention: float32 [4, 768, 768], P(None, 'fsdp')
- updated_expand: float32 [768, 3072], P('fsdp')
- updated_contract: float32 [3072, 768], P('fsdp')
- updated_vectors: float32 [12, 768], P(None, 'fsdp')
- average_attention: float32 [4, 768, 768], P(None, 'fsdp')
- average_expand: float32 [768, 3072], P('fsdp')
- average_contract: float32 [3072, 768], P('fsdp')
- average_vectors: float32 [12, 768], P(None, 'fsdp')
- variance_attention: float32 [4, 768, 768], P(None, 'fsdp')
- variance_expand: float32 [768, 3072], P('fsdp')
- variance_contract: float32 [3072, 768], P('fsdp')
- variance_vectors: float32 [12, 768], P(None, 'fsdp')
All inputs are finite; a program needn't handle non-finite values.
Results may differ from a plain program's by a relative error of at most 0.0095.
The roundings to bfloat16 on the way count: a program that leaves them out, or rounds other values in their place, can miss the bound.
Values may be sent and summed in bfloat16 or wider, within the bound.
A program may use at most 320 MiB of HBM per device.

v0:
```python
import functools

import jax
import jax.numpy as jnp
from jax import lax
from jax.experimental import pallas as pl
from jax.experimental.pallas import tpu as pltpu
from jax.sharding import PartitionSpec as P

HEADS = 12
norm_eps = 1e-05
beta_one = 0.9
beta_two = 0.999
adam_eps = 1e-08
adam_count = 5.0
rate_matrix = 0.02
rate_vector = 0.1
decay_matrix = 0.1
score_scale = 0.125
VMEM_LIMIT = 60 << 20
MESH = pl.DeviceIdType.MESH
BF = jnp.bfloat16
F32 = jnp.float32


def nt(left, right):
    return lax.dot_general(left, right, (((1,), (1,)), ((), ())), preferred_element_type=F32)


def nn(left, right):
    return lax.dot_general(left, right, (((1,), (0,)), ((), ())), preferred_element_type=F32)


def tn(left, right):
    return lax.dot_general(left, right, (((0,), (0,)), ((), ())), preferred_element_type=F32)


def vmem():
    return pl.BlockSpec(memory_space=pltpu.VMEM)


def normalize(values):
    center = values - jnp.mean(values, axis=-1, keepdims=True)
    inverse = lax.rsqrt(jnp.mean(center * center, axis=-1, keepdims=True) + norm_eps)
    return center * inverse, inverse


def norm_back(upstream, normed, inverse, gain):
    scaled = upstream * gain
    inner = (
        scaled
        - jnp.mean(scaled, axis=-1, keepdims=True)
        - normed * jnp.mean(scaled * normed, axis=-1, keepdims=True)
    )
    return (inverse * inner, jnp.sum(upstream * normed, axis=0), jnp.sum(upstream, axis=0))


def adam_update(weight, gradient, first, second, rate, decay):
    first_new = beta_one * first + (1.0 - beta_one) * gradient
    second_new = beta_two * second + (1.0 - beta_two) * gradient * gradient
    first_hat = first_new / (1.0 - beta_one**adam_count)
    second_hat = second_new / (1.0 - beta_two**adam_count)
    updated = weight - rate * (first_hat / (jnp.sqrt(second_hat) + adam_eps) + decay * weight)
    return (updated, first_new, second_new)


class Place:
    def __init__(self, sizes):
        self.nd, self.nf, self.ns = sizes
        self.nh = self.nd // 2
        self.dp = lax.axis_index("dp")
        self.x = lax.axis_index("fsdp")
        self.z = lax.axis_index("seq")
        self.core = lax.rem(self.dp, 2)
        self.hi = self.dp // 2

    def sibling(self):
        return {"dp": self.hi * 2 + 1 - self.core}

    def x_peer(self, k):
        return {"fsdp": lax.rem(self.x + k, self.nf)}

    def y_hi(self, k):
        return lax.rem(self.hi + k, self.nh)

    def y_peer(self, k):
        return {"dp": self.y_hi(k) * 2 + self.core}

    def z_at(self, k):
        return lax.rem(self.z + k + self.ns, self.ns)

    def z_peer(self, k):
        return {"seq": self.z_at(k)}

    def everyone(self):
        out = [self.sibling()]
        out += [self.x_peer(k) for k in range(1, self.nf)]
        out += [self.y_peer(k) for k in range(1, self.nh)]
        out += [self.z_peer(k) for k in range(1, self.ns)]
        return out

    def barrier(self):
        sem = pltpu.get_barrier_semaphore()
        peers = self.everyone()
        for peer in peers:
            pl.semaphore_signal(sem, inc=1, device_id=peer, device_id_type=MESH)
        pl.semaphore_wait(sem, len(peers))


def remote(src, dst, send, recv, peer):
    return pltpu.make_async_remote_copy(
        src_ref=src, dst_ref=dst, send_sem=send, recv_sem=recv, device_id=peer, device_id_type=MESH
    )


def front_kernel(
    sizes, frames_ref, vec_ref, aw_ref, ew_ref, cw_ref,
    a_out, e_ref, c_ref, vec_out, ht_out, q_out, k_out, v_out, ctx_out, lse_ref,
    a_ref, v_buf, h_ref, ht, q_buf, k_buf, v_buf2, ctx_buf, af, ef, eb, cb, kept, stat,
    ls, xs, xr, ys, yr, s1s, s1r, s2s, s2r, vs, vr, rs, hs, hr,
):
    at = Place(sizes)
    nf, nh, ns = at.nf, at.nh, at.ns
    rows, width = frames_ref.shape
    shard = aw_ref.shape[1]
    half = shard // 2
    deep = cb.shape[0]
    b0 = lax.rem(at.z, 2)
    b1 = at.z // 2

    def load(i, src, dst):
        return pltpu.make_async_copy(src, dst, ls.at[i])

    loads = [
        load(0, aw_ref.at[pl.ds(0, 3)], af.at[pl.ds(0, 3)]),
        load(1, aw_ref.at[pl.ds(3, 1)], af.at[pl.ds(3, 1)]),
        load(2, ew_ref, ef),
        load(3, cw_ref, af),
    ]
    for copy in loads[:3]:
        copy.start()
    at.barrier()
    v_buf[at.x] = jnp.zeros(v_buf.shape[1:], BF)
    v_buf[at.x, 0 : vec_ref.shape[0], :] = vec_ref[...].astype(BF)
    vec_copies = []
    for k in range(1, nf):
        copy = remote(v_buf.at[at.x], v_buf.at[at.x], vs.at[k], vr.at[k], at.x_peer(k))
        copy.start()
        vec_copies.append(copy)

    def view(chunk, j, hi, core, own=False):
        if chunk < 2:
            first, count = ((0, 3), (3, 1))[chunk]
            cols = width // nh
            return a_ref.at[
                pl.ds(first, count),
                pl.ds(pl.multiple_of(j * shard + core * half, 16), half),
                pl.ds(pl.multiple_of(hi * cols, 128), cols),
            ]
        ref, stage, size = ((e_ref, eb, shard), (c_ref, cb, deep))[chunk - 2]
        cols = ref.shape[1] // nh
        start = core * (size // 2)
        if own:
            ref = stage
        else:
            start = j * size + start
        return ref.at[
            pl.ds(pl.multiple_of(start, 16), size // 2),
            pl.ds(pl.multiple_of(hi * cols, 128), cols),
        ]

    own = pl.multiple_of(at.x * shard, 16)
    x_copies = {}

    def send_chunk(chunk):
        for k in range(1, nf):
            copy = remote(
                view(chunk, at.x, at.hi, at.core, True), view(chunk, at.x, at.hi, at.core),
                xs.at[chunk, k], xr.at[chunk, k], at.x_peer(k),
            )
            copy.start()
            x_copies[chunk, k] = copy

    loads[0].wait()
    for u in range(3):
        a_ref[u, pl.ds(own, shard), :] = af[u].astype(BF)
    send_chunk(0)
    normed, _ = normalize(frames_ref[...])
    for copy in vec_copies:
        copy.wait()
    vec = jnp.concatenate([v_buf[j] for j in range(nf)], axis=1).astype(F32)
    vec_out[...] = vec
    mine = pl.ds(pl.multiple_of(at.z * rows, 128), rows)
    hidden = (normed * vec[0:1] + vec[1:2]).astype(BF)
    h_ref[mine, :] = hidden

    def block(b):
        return h_ref.at[pl.ds(pl.multiple_of(b * rows, 128), rows), :]

    def to_right(b):
        return remote(block(b), block(b), rs.at[b], hr.at[b], {"seq": at.z + 1})

    def to_left(b):
        return remote(block(b), block(b), hs.at[b], hr.at[b], {"seq": at.z - 1})

    @pl.when(at.z < ns - 1)
    def _():
        to_right(at.z).start()

    @pl.when(at.z > 0)
    def _():
        to_left(at.z).start()

    loads[1].wait()
    a_ref[3, pl.ds(own, shard), :] = af[3].astype(BF)
    loads[3].start()
    send_chunk(1)
    loads[2].wait()
    eb[...] = ef[...].astype(BF)
    send_chunk(2)
    loads[3].wait()
    for u in range(4):
        cb[pl.ds(u * shard, shard), :] = af[u].astype(BF)
    send_chunk(3)
    stores = [
        load(4, eb, e_ref.at[pl.ds(own, shard), :]),
        load(5, cb, c_ref.at[pl.ds(pl.multiple_of(at.x * deep, 16), deep), :]),
    ]
    for copy in stores:
        copy.start()
    ht[:, mine] = hidden.T

    def first_copy(chunk, k):
        j = lax.rem(at.x - k + nf, nf)
        piece = view(chunk, j, at.hi, at.core)
        return remote(piece, piece, s1s.at[chunk, k], s1r.at[chunk, k], at.sibling())

    def y_copy(chunk, k, m):
        j = lax.rem(at.x - k + nf, nf)
        piece = view(chunk, j, at.hi, at.core)
        return remote(piece, piece, ys.at[chunk, k, m], yr.at[chunk, k, m], at.y_peer(m))

    def second_copy(chunk, k, m):
        j = lax.rem(at.x - k + nf, nf)
        piece = view(chunk, j, lax.rem(at.hi - m + nh, nh), at.core)
        return remote(piece, piece, s2s.at[chunk, k, m], s2r.at[chunk, k, m], at.sibling())

    def forward(chunk):
        for k in range(1, nf):
            x_copies[chunk, k].wait_recv()
            first_copy(chunk, k).start()
            for m in range(1, nh):
                y_copy(chunk, k, m).start()

    def relay(chunk):
        for k in range(1, nf):
            for m in range(1, nh):
                y_copy(chunk, k, m).wait_recv()
                second_copy(chunk, k, m).start()

    def arrived(chunk):
        for k in range(1, nf):
            first_copy(chunk, k).wait_recv()
            for m in range(1, nh):
                second_copy(chunk, k, m).wait_recv()

    def rows_of(b):
        part = pl.ds(pl.multiple_of(b * rows, 128), rows)
        k_buf[part, :] = nn(h_ref[part, :], a_ref[1]).astype(BF)
        v_buf2[part, :] = (nn(h_ref[part, :], a_ref[2]) + vec[3:4]).astype(BF)

    def turn(b):
        part = pl.ds(pl.multiple_of(b * rows, 128), rows)
        ht[:, part] = h_ref[part, :].T

    def hop(s):
        b = at.z - s
        d = at.z + s

        @pl.when(b >= 0)
        def _():
            to_right(b).wait_recv()

            @pl.when(at.z < ns - 1)
            def _():
                to_right(b).start()

        @pl.when(d < ns)
        def _():
            to_left(d).wait_recv()

            @pl.when(at.z > 0)
            def _():
                to_left(d).start()

    lane = lax.broadcasted_iota(jnp.int32, (rows, 128), 1)
    lo = lane < 64

    def scores(p, h, b):
        col = pl.ds(pl.multiple_of(p * 128, 128), 128)
        part = pl.ds(pl.multiple_of(b * rows, 128), rows)
        q2 = q_buf[:, col]
        mask = lo if h == 0 else jnp.logical_not(lo)
        s = nt(jnp.where(mask, q2, jnp.zeros_like(q2)), k_buf[part, col]) * score_scale
        largest = jnp.max(s, axis=-1, keepdims=True)
        e = jnp.exp(s - largest)
        return e, largest, jnp.sum(e, axis=-1, keepdims=True)

    assert ns == 4
    blocks = (at.z, at.z + 1 - 2 * b0, 2 - b1, 3 - 3 * b1)

    def begin(i):
        b = blocks[i]
        rows_of(b)

        def pair(p, carry):
            found = []
            for h in range(2):
                e, largest, total = scores(p, h, b)
                kept[i, 2 * p + h] = e
                found += [largest, total]
            stat[i, p] = jnp.where(
                lo, jnp.where(lane < 32, found[0], found[1]), jnp.where(lane < 96, found[2], found[3])
            )
            return carry

        lax.fori_loop(0, width // 128, pair, 0)

    forward(0)
    hop(1)
    forward(1)
    relay(0)
    arrived(0)
    q_buf[...] = (nn(h_ref[mine, :], a_ref[0]) + vec[2:3]).astype(BF)
    stores.append(load(6, q_buf, q_out))
    stores[-1].start()
    begin(0)
    hop(2)
    begin(1)
    turn(blocks[1])
    relay(1)
    forward(2)
    begin(2)
    turn(blocks[2])
    hop(3)
    rows_of(blocks[3])
    turn(blocks[3])
    arrived(1)
    for i, (src, dst) in enumerate(((a_ref, a_out), (ht, ht_out), (k_buf, k_out), (v_buf2, v_out))):
        stores.append(load(7 + i, src, dst))
        stores[-1].start()
    forward(3)
    relay(2)

    def pair(p, carry):
        col = pl.ds(pl.multiple_of(p * 128, 128), 128)
        ctx, lse = [], []
        for h in range(2):
            e, peak, count = scores(p, h, blocks[3])
            peaks = [stat[i, p][:, 64 * h : 64 * h + 1] for i in range(3)] + [peak]
            counts = [stat[i, p][:, 64 * h + 32 : 64 * h + 33] for i in range(3)] + [count]
            largest = functools.reduce(jnp.maximum, peaks)
            shares = [jnp.exp(each - largest) for each in peaks]
            total = sum(share * each for share, each in zip(shares, counts))
            inverse = 1.0 / total
            out = None
            for i in range(4):
                part = pl.ds(pl.multiple_of(blocks[i] * rows, 128), rows)
                found = kept[i, 2 * p + h] if i < 3 else e
                term = nn((found * (shares[i] * inverse)).astype(BF), v_buf2[part, col])
                out = term if out is None else out + term
            ctx.append(out)
            lse.append(largest + jnp.log(total))
        ctx_buf[:, col] = jnp.where(lo, ctx[0], ctx[1])
        lse_ref[p] = jnp.where(lo, lse[0], lse[1])

        @pl.when(p == 1)
        def _():
            relay(3)

        return carry

    lax.fori_loop(0, width // 128, pair, 0)
    stores.append(load(11, ctx_buf, ctx_out))
    stores[-1].start()
    arrived(2)
    arrived(3)
    for copy in stores:
        copy.wait()
    for copy in x_copies.values():
        copy.wait_send()
    for chunk in range(4):
        for k in range(1, nf):
            first_copy(chunk, k).wait_send()
            for m in range(1, nh):
                y_copy(chunk, k, m).wait_send()
                second_copy(chunk, k, m).wait_send()
    for b in range(ns):
        @pl.when(jnp.logical_and(b <= at.z, at.z < ns - 1))
        def _():
            to_right(b).wait_send()

        @pl.when(jnp.logical_and(b >= at.z, at.z > 0))
        def _():
            to_left(b).wait_send()


def front_all(sizes, frames, vec, aw, ew, cw):
    nd, nf, ns = sizes
    nh = nd // 2
    rows, width = frames.shape
    shard, full = ew.shape
    deep = cw.shape[0]
    every = rows * ns
    dma = pltpu.SemaphoreType.DMA
    anywhere = pl.BlockSpec(memory_space=pl.ANY)
    return pl.pallas_call(
        functools.partial(front_kernel, sizes),
        out_shape=(
            jax.ShapeDtypeStruct((4, width, width), BF),
            jax.ShapeDtypeStruct((width, full), BF),
            jax.ShapeDtypeStruct((deep * nf, width), BF),
            jax.ShapeDtypeStruct((16, width), F32),
            jax.ShapeDtypeStruct((width, every), BF),
            jax.ShapeDtypeStruct((rows, width), BF),
            jax.ShapeDtypeStruct((every, width), BF),
            jax.ShapeDtypeStruct((every, width), BF),
            jax.ShapeDtypeStruct((rows, width), F32),
            jax.ShapeDtypeStruct((width // 128, rows, 128), F32),
        ),
        in_specs=[vmem(), vmem(), anywhere, anywhere, anywhere],
        out_specs=(anywhere, anywhere, anywhere, vmem()) + (anywhere,) * 5 + (vmem(),),
        scratch_shapes=[
            pltpu.VMEM((4, width, width), BF),
            pltpu.VMEM((nf, 16, vec.shape[1]), BF),
            pltpu.VMEM((every, width), BF),
            pltpu.VMEM((width, every), BF),
            pltpu.VMEM((rows, width), BF),
            pltpu.VMEM((every, width), BF),
            pltpu.VMEM((every, width), BF),
            pltpu.VMEM((rows, width), F32),
            pltpu.VMEM((4, shard, width), F32),
            pltpu.VMEM((shard, full), F32),
            pltpu.VMEM((shard, full), BF),
            pltpu.VMEM((deep, width), BF),
            pltpu.VMEM((ns - 1, width // 64, rows, rows), F32),
            pltpu.VMEM((ns - 1, width // 128, rows, 128), F32),
            dma((12,)),
            dma((4, nf)), dma((4, nf)),
            dma((4, nf, nh)), dma((4, nf, nh)),
            dma((4, nf)), dma((4, nf)),
            dma((4, nf, nh)), dma((4, nf, nh)),
            dma((nf,)), dma((nf,)),
            dma((ns,)), dma((ns,)), dma((ns,)),
        ],
        name="front",
        compiler_params=pltpu.CompilerParams(
            collective_id=0, has_side_effects=True, vmem_limit_bytes=67043328
        ),
    )(frames, vec, aw, ew, cw.reshape(aw.shape))


def back_kernel(
    sizes, q_ref, k_ref, v_ref, dc_ref, ctx_ref, lse_ref, ht_ref, w_ref, gm_ref, frames_ref,
    vec_ref, gv_ref, gc_ref, ge_ref, go_ref,
    oc_ref, oe_ref, oa_ref, ig_ref, ov_ref,
    ga, own, rc, rx, ry, rz, ri, dkt, dvt, dqa, dhs, dra, drb, drc, vb, vx, vy, vz,
    os, cs, cr, xs, xr, ys, yr, zs, zr, zis, zir, gs, gr, ays, ayr, acs, acr,
    das, dar, dbs, dbr, dcs, dcr, vs, vr,
):
    at = Place(sizes)
    nf, nh, ns = at.nf, at.nh, at.ns
    rows, width = q_ref.shape
    q = rc.shape[5]
    cols = width // nh
    per = cols // 128
    chunks = rc.shape[0]
    split = chunks // (3 * per)
    half = q * split
    group = per * split
    b0 = lax.rem(at.z, 2)
    b1 = at.z // 2
    at.barrier()

    def strip(core, r):
        return pl.ds(pl.multiple_of(core * half + r * q, 16), q)

    def lanes(s, hi):
        return pl.ds(pl.multiple_of(hi * cols + s * 128, 128), 128)

    def place_of(n):
        return n // group, lax.rem(n, group) // split, lax.rem(n, split)

    for s in range(per):
        for hi in range(nh):
            for part in range(2):
                for r in range(split):
                    pltpu.make_async_copy(
                        go_ref.at[:, pl.ds(part * half + r * q, q), pl.ds(hi * cols + s * 128, 128)],
                        ga.at[s, r, hi, :, part, 1, 1],
                        os.at[4],
                    ).start()

    def own_whole(slot):
        return pltpu.make_async_copy(own.at[slot], own.at[slot], os.at[slot])

    def c_whole(n):
        return remote(rc.at[n], rc.at[n], cs.at[n], cr.at[n], at.sibling())

    def c_send(n):
        slot = lax.rem(n, 4)
        g, s, r = place_of(n)

        @pl.when(n < group)
        def _():
            for hi in range(nh):
                for u in range(4):
                    block = lanes(s, hi)
                    remote(
                        gc_ref.at[:, u, strip(1 - at.core, r), block],
                        rc.at[n, hi, :, u // 2, u % 2], cs.at[n], cr.at[n], at.sibling(),
                    ).start()
                    pltpu.make_async_copy(
                        gc_ref.at[:, u, strip(at.core, r), block],
                        own.at[slot, hi, :, u // 2, u % 2], os.at[slot],
                    ).start()

        @pl.when(jnp.logical_and(n >= group, n < 2 * group))
        def _():
            for hi in range(nh):
                for u in range(4):
                    block = pl.ds(pl.multiple_of(u * width + hi * cols + s * 128, 128), 128)
                    remote(
                        ge_ref.at[:, strip(1 - at.core, r), block],
                        rc.at[n, hi, :, u // 2, u % 2], cs.at[n], cr.at[n], at.sibling(),
                    ).start()
                    pltpu.make_async_copy(
                        ge_ref.at[:, strip(at.core, r), block],
                        own.at[slot, hi, :, u // 2, u % 2], os.at[slot],
                    ).start()

        @pl.when(jnp.logical_and(n >= 2 * group, n < chunks))
        def _():
            remote(
                ga.at[s, r, :, :, 1 - at.core], rc.at[n], cs.at[n], cr.at[n], at.sibling()
            ).start()

    def x_copy(n, k):
        peer = lax.rem(at.x + k, nf)
        return remote(rc.at[n, :, peer], rx.at[n, k - 1], xs.at[n, k - 1], xr.at[n, k - 1], at.x_peer(k))

    def y_copy(n, m):
        return remote(
            rx.at[n, 0, at.y_hi(m)], ry.at[n, m - 1], ys.at[n, m - 1], yr.at[n, m - 1], at.y_peer(m)
        )

    assert ns == 4
    outer = b0 == b1
    inner = b0 != b1
    near = {"seq": at.z + 1 - 2 * b0}
    across = {"seq": 3 - at.z}

    def z_copy(n):
        return remote(ry.at[n, 0], rz.at[n], zs.at[n], zr.at[n], near)

    def zi_copy(n):
        return remote(ry.at[n, 0], ri.at[n], zis.at[n], zir.at[n], across)

    def by_group(n, act):
        g, s, r = place_of(n)

        for which in range(3):
            @pl.when(g == which)
            def _(which=which):
                def place(hi, ua, ub):
                    if which == 1:
                        start = (2 * ua + ub) * width + hi * cols + s * 128
                        return oe_ref.at[strip(at.core, r), pl.ds(pl.multiple_of(start, 128), 128)]
                    ref = oc_ref if which == 0 else oa_ref
                    return ref.at[ua, ub, strip(at.core, r), lanes(s, hi)]

                act(place)

    def g_whole(n):
        return remote(ry.at[n, 0], ry.at[n, 0], gs.at[n], gr.at[n], near)

    def ay_whole(n, m):
        return remote(ry.at[n, 0], ry.at[n, 0], ays.at[n, m - 1], ayr.at[n, m - 1], at.y_peer(m))

    def ac_whole(n):
        return remote(rx.at[n, 0], rx.at[n, 0], acs.at[n], acr.at[n], at.sibling())

    def g_start(n, total):
        def act(place):
            for u in range(4):
                spot = place(at.hi, u // 2, u % 2)
                spot[...] = total[u // 2, u % 2]
                remote(spot, spot, gs.at[n], gr.at[n], near).start()

        by_group(n, act)

    def ay_start(n):
        def act(place):
            for m in range(1, nh):
                for u in range(4):
                    spot = place(at.hi, u // 2, u % 2)
                    remote(spot, spot, ays.at[n, m - 1], ayr.at[n, m - 1], at.y_peer(m)).start()

        by_group(n, act)

    def ac_start(n):
        def act(place):
            for hi in range(nh):
                for u in range(4):
                    spot = place(hi, u // 2, u % 2)
                    remote(spot, spot, acs.at[n], acr.at[n], at.sibling()).start()

        by_group(n, act)

    def plus(left, right):
        if nf == 2:
            return left + right
        return (left.astype(F32) + right.astype(F32)).astype(BF)

    def stage_c(n):
        c_whole(n).wait_recv()
        slot = lax.rem(n, 4)
        _, s, r = place_of(n)

        @pl.when(n < 2 * group)
        def _():
            own_whole(slot).wait()

            def add(i, carry):
                hi, j = i // nf, lax.rem(i, nf)
                rc[n, hi, j] = plus(rc[n, hi, j], own[slot, hi, j])
                return carry

            lax.fori_loop(0, nh * nf, add, 0)

        @pl.when(n >= 2 * group)
        def _():
            def add(i, carry):
                hi, j = i // nf, lax.rem(i, nf)
                rc[n, hi, j] = plus(rc[n, hi, j], ga[s, r, hi, j, at.core])
                return carry

            lax.fori_loop(0, nh * nf, add, 0)

        for k in range(1, nf):
            x_copy(n, k).start()

    def stage_x(n):
        for k in range(1, nf):
            x_copy(n, k).wait_recv()

        def add(hi, carry):
            if nf == 2:
                rx[n, 0, hi] = rc[n, hi, at.x] + rx[n, 0, hi]
            else:
                total = rc[n, hi, at.x].astype(F32)
                for k in range(nf - 1):
                    total += rx[n, k, hi].astype(F32)
                rx[n, 0, hi] = total.astype(BF)
            return carry

        lax.fori_loop(0, nh, add, 0)
        for m in range(1, nh):
            y_copy(n, m).start()

    def stage_y(n):
        for m in range(1, nh):
            y_copy(n, m).wait_recv()
        total = rx[n, 0, at.hi]
        for m in range(nh - 1):
            total = plus(total, ry[n, m])
        ry[n, 0] = total

        @pl.when(outer)
        def _():
            z_copy(n).start()

    def stage_z(n):
        @pl.when(inner)
        def _():
            z_copy(n).wait_recv()
            ry[n, 0] = plus(ry[n, 0], rz[n])
            zi_copy(n).start()

    def stage_zi(n):
        @pl.when(inner)
        def _():
            zi_copy(n).wait_recv()
            g_start(n, plus(ry[n, 0], ri[n]))

    def stage_g(n):
        @pl.when(outer)
        def _():
            g_whole(n).wait_recv()

        ay_start(n)

    def stage_ay(n):
        for m in range(1, nh):
            ay_whole(n, m).wait_recv()
        ac_start(n)

    lo = lax.broadcasted_iota(jnp.int32, (rows, 128), 1) < 64
    pairs = width // 128

    def unit(index):
        i, p = index // pairs, lax.rem(index, pairs)
        there = 1 - b1 - i + 2 * i * b1
        keys = pl.ds(pl.multiple_of(there * (2 * rows), 128), 2 * rows)
        col = pl.ds(pl.multiple_of(p * 128, 128), 128)
        k2 = k_ref[keys, col]
        v2 = v_ref[keys, col]
        q2 = q_ref[:, col]
        dc2 = dc_ref[:, col]
        both = dc2.astype(F32) * ctx_ref[:, col]
        lse2 = lse_ref[p]
        dq, dk, dv = [], None, None
        for h in range(2):
            mask = lo if h == 0 else jnp.logical_not(lo)
            qm = jnp.where(mask, q2, jnp.zeros_like(q2))
            dmask = jnp.where(mask, dc2, jnp.zeros_like(q2))
            lse = lse2[:, 0:1] if h == 0 else lse2[:, 64:65]
            dot = jnp.sum(jnp.where(mask, both, 0.0), axis=-1, keepdims=True)
            probs = jnp.exp(nt(qm, k2) * score_scale - lse)
            slopes = nt(dmask, v2)
            dscore = (probs * (slopes - dot) * score_scale).astype(BF)
            dq.append(nn(dscore, k2))
            a = nn(dmask.T, probs.astype(BF))
            b = nn(qm.T, dscore)
            dv = a if dv is None else dv + a
            dk = b if dk is None else dk + b
        dq2 = jnp.where(lo, dq[0], dq[1])

        @pl.when(i == 0)
        def _():
            dqa[:, col] = dq2

        @pl.when(i > 0)
        def _():
            dqa[:, col] += dq2

        dkt[col, keys] = dk.astype(BF)
        dvt[col, keys] = dv.astype(BF)

    def weights(s):
        frames = pl.ds(pl.multiple_of(at.z * rows, 128), rows)
        for hi in range(nh):
            col = lanes(s, hi)
            dq2 = dqa[:, col]
            vb[2, 0:1, col] = jnp.sum(dq2, axis=0, keepdims=True)
            dq2 = dq2.astype(BF)
            dk2 = dkt[col, :]
            dv2 = dvt[col, :]
            for j in range(nf):
                for part in range(2):
                    for r in range(split):
                        here = pl.ds((2 * j + part) * half + r * q, q)
                        ga[s, r, hi, j, part, 0, 0] = nn(ht_ref[here, frames], dq2).astype(BF)
                        ga[s, r, hi, j, part, 0, 1] = nt(ht_ref[here, :], dk2).astype(BF)
                        ga[s, r, hi, j, part, 1, 0] = nt(ht_ref[here, :], dv2).astype(BF)

    pieces = 16
    per_step = 2
    lag = 2
    low = 1 - b1

    def part_of(t):
        return pl.ds(pl.multiple_of(t * (width // pieces), 16), width // pieces)

    def da_copy(t):
        return remote(
            dhs.at[pl.ds(low, 3), part_of(t)], dra.at[:, part_of(t)], das.at[t], dar.at[t], near
        )

    def db_copy(t):
        return remote(
            dhs.at[pl.ds(2 * low, 2), part_of(t)], drb.at[:, part_of(t)], dbs.at[t], dbr.at[t], across
        )

    def dc_copy(t):
        return remote(dhs.at[3 * b1, part_of(t)], drc.at[part_of(t)], dcs.at[t], dcr.at[t], near)

    def d_stage(i, t):
        part = part_of(t)
        if i == 0:
            @pl.when(outer)
            def _():
                da_copy(t).start()
        elif i == 1:
            @pl.when(inner)
            def _():
                da_copy(t).wait_recv()
                for j in range(3):
                    dhs[low + j, part] = dhs[low + j, part] + dra[j, part]
                db_copy(t).start()
        elif i == 2:
            @pl.when(inner)
            def _():
                db_copy(t).wait_recv()
                for j in range(2):
                    dhs[2 * b1 + j, part] = dhs[2 * b1 + j, part] + drb[j, part]
                dc_copy(t).start()
        else:
            @pl.when(outer)
            def _():
                dc_copy(t).wait_recv()

    def spread(i):
        there = 1 - b1 - i + 2 * i * b1
        for ub in range(2):
            part = pl.ds(pl.multiple_of((2 * there + ub) * rows, 128), rows)
            dhs[2 * there + ub] = (nn(w_ref[1], dkt[:, part]) + nn(w_ref[2], dvt[:, part])).astype(BF)

    def first_norm():
        @pl.when(inner)
        def _():
            drc[...] = jnp.zeros_like(drc)

        total = dhs[at.z].astype(F32) + nt(w_ref[0], dqa[...].astype(BF))
        total += drc[...].astype(F32)
        total = total.T
        normed, inverse = normalize(frames_ref[...])
        scaled = total * vec_ref[0:1, :]
        centred = (
            scaled
            - jnp.mean(scaled, axis=-1, keepdims=True)
            - normed * jnp.mean(scaled * normed, axis=-1, keepdims=True)
        )
        ig_ref[...] = gm_ref[...] + inverse * centred
        vb[1] = gv_ref[...]
        vb[1, 0:1, :] = jnp.sum(total * normed, axis=0, keepdims=True)
        vb[1, 1:2, :] = jnp.sum(total, axis=0, keepdims=True)
        vb[1, 2:3, :] = vb[2, 0:1, :]

    def v_core():
        return remote(vb.at[1], vb.at[0], vs.at[0], vr.at[0], at.sibling())

    def v_x(k):
        return remote(vx.at[at.x], vx.at[at.x], vs.at[k], vr.at[k], at.x_peer(k))

    def v_y(m):
        return remote(vy.at[at.hi], vy.at[at.hi], vs.at[nf + m], vr.at[nf + m], at.y_peer(m))

    def v_z(k):
        return remote(
            vz.at[at.z], vz.at[at.z], vs.at[nf + nh + k], vr.at[nf + nh + k], at.z_peer(k)
        )

    def v_step(i):
        if i == 0:
            v_core().start()
        elif i == 1:
            v_core().wait_recv()
            vx[at.x] = vb[0] + vb[1]
            for k in range(1, nf):
                v_x(k).start()
        elif i == 2:
            for k in range(1, nf):
                v_x(k).wait_recv()
            total = vx[0]
            for j in range(1, nf):
                total += vx[j]
            vy[at.hi] = total
            for m in range(1, nh):
                v_y(m).start()
        elif i == 3:
            for m in range(1, nh):
                v_y(m).wait_recv()
            total = vy[0]
            for j in range(1, nh):
                total += vy[j]
            vz[at.z] = total
            for k in range(1, ns):
                v_z(k).start()
        else:
            for k in range(1, ns):
                v_z(k).wait_recv()
            total = vz[0]
            for j in range(1, ns):
                total += vz[j]
            ov_ref[...] = total

    ready = group
    each = -(-2 * pairs // ready)
    done = [-(-pairs * (i + 1) // each) - 1 for i in range(2)]
    away = done[1] + 1
    norm = max(away + (pieces - 1) // per_step + 4, chunks - 2)
    stages = (stage_x, stage_y, stage_z, stage_zi, stage_g, stage_ay)
    last = max(chunks + lag * len(stages), norm + 6)
    for n in range(4):
        c_send(n)

    def step(n, carry):
        for k in range(2):
            @pl.when(2 * n + k < 2 * group)
            def _(k=k):
                stage_c(2 * n + k)

                @pl.when(2 * n + k + 4 < 2 * group)
                def _():
                    c_send(2 * n + k + 4)

        @pl.when(jnp.logical_and(n >= ready + 1, n < ready + 1 + per))
        def _():
            for r in range(split):
                stage_c(2 * group + (n - ready - 1) * split + r)

        @pl.when(n < ready)
        def _():
            def one(k, carry):
                @pl.when(n * each + k < 2 * pairs)
                def _():
                    unit(n * each + k)

                return carry

            lax.fori_loop(0, each, one, 0)

        @pl.when(jnp.logical_or(n == done[0], n == done[1]))
        def _():
            spread(n // done[1])

        @pl.when(n == norm)
        def _():
            first_norm()

        @pl.when(n == ready)
        def _():
            whole = ga.at[:, :, :, :, :, 1, 1]
            pltpu.make_async_copy(whole, whole, os.at[4]).wait()

        @pl.when(jnp.logical_and(n >= ready, n < ready + per))
        def _():
            weights(n - ready)
            for r in range(split):
                c_send(2 * group + (n - ready) * split + r)

        for i, stage in enumerate(stages):
            @pl.when(jnp.logical_and(n >= lag * i, n < chunks + lag * i))
            def _(i=i, stage=stage):
                stage(n - lag * i)

        for i in range(4):
            first = away + i

            @pl.when(jnp.logical_and(n >= first, n < first + pieces // per_step))
            def _(i=i, first=first):
                for t in range(per_step):
                    d_stage(i, (n - first) * per_step + t)

        for i in range(5):
            @pl.when(n == norm + i)
            def _(i=i):
                v_step(i)

        return carry

    lax.fori_loop(0, last, step, 0)
    for n in range(chunks):
        ac_whole(n).wait()

    def drain(n, carry):
        c_whole(n).wait_send()

        @pl.when(outer)
        def _():
            z_copy(n).wait_send()

        @pl.when(inner)
        def _():
            zi_copy(n).wait_send()
            g_whole(n).wait_send()

        for k in range(1, nf):
            x_copy(n, k).wait_send()
        for m in range(1, nh):
            y_copy(n, m).wait_send()
            ay_whole(n, m).wait_send()
        return carry

    lax.fori_loop(0, chunks, drain, 0)

    @pl.when(outer)
    def _():
        def sent(t, carry):
            da_copy(t).wait_send()
            return carry

        lax.fori_loop(0, pieces, sent, 0)

    @pl.when(inner)
    def _():
        def sent(t, carry):
            db_copy(t).wait_send()
            dc_copy(t).wait_send()
            return carry

        lax.fori_loop(0, pieces, sent, 0)

    for k in range(1, ns):
        v_z(k).wait_send()
    for k in range(1, nf):
        v_x(k).wait_send()
    for m in range(1, nh):
        v_y(m).wait_send()
    v_core().wait_send()


def back_all(sizes, q, k, v, dc, ctx, lse, ht, w, gm, frames, vec, gv, gc, ge, go):
    nd, nf, ns = sizes
    nh = nd // 2
    rows, width = q.shape
    shard = go.shape[1]
    half = shard // 2
    every = k.shape[0]
    split = 2 if half % 32 == 0 else 1
    strip = half // split
    per = width // nh // 128
    chunks = 3 * per * split
    xn, yn = max(nf - 1, 1), max(nh - 1, 1)
    dma = pltpu.SemaphoreType.DMA
    anywhere = pl.BlockSpec(memory_space=pl.ANY)
    return pl.pallas_call(
        functools.partial(back_kernel, sizes),
        out_shape=(
            jax.ShapeDtypeStruct((2, 2, shard, width), BF),
            jax.ShapeDtypeStruct((shard, 4 * width), BF),
            jax.ShapeDtypeStruct((2, 2, shard, width), BF),
            jax.ShapeDtypeStruct((rows, width), F32),
            jax.ShapeDtypeStruct((16, width), F32),
        ),
        in_specs=[vmem()] * 12 + [anywhere] * 3,
        out_specs=(vmem(),) * 5,
        scratch_shapes=[
            pltpu.VMEM((per, split, nh, nf, 2, 2, 2, strip, 128), BF),
            pltpu.VMEM((4, nh, nf, 2, 2, strip, 128), BF),
            pltpu.VMEM((chunks, nh, nf, 2, 2, strip, 128), BF),
            pltpu.VMEM((chunks, xn, nh, 2, 2, strip, 128), BF),
            pltpu.VMEM((chunks, yn, 2, 2, strip, 128), BF),
            pltpu.VMEM((chunks, 2, 2, strip, 128), BF),
            pltpu.VMEM((chunks, 2, 2, strip, 128), BF),
            pltpu.VMEM((width, every), BF),
            pltpu.VMEM((width, every), BF),
            pltpu.VMEM((rows, width), F32),
            pltpu.VMEM((ns, width, rows), BF),
            pltpu.VMEM((3, width, rows), BF),
            pltpu.VMEM((2, width, rows), BF),
            pltpu.VMEM((width, rows), BF),
            pltpu.VMEM((3, 16, width), F32),
            pltpu.VMEM((nf, 16, width), F32),
            pltpu.VMEM((nh, 16, width), F32),
            pltpu.VMEM((ns, 16, width), F32),
            dma((5,)),
            dma((chunks,)), dma((chunks,)),
            dma((chunks, xn)), dma((chunks, xn)),
            dma((chunks, yn)), dma((chunks, yn)),
            dma((chunks,)), dma((chunks,)),
            dma((chunks,)), dma((chunks,)),
            dma((chunks,)), dma((chunks,)),
            dma((chunks, yn)), dma((chunks, yn)),
            dma((chunks,)), dma((chunks,)),
            dma((16,)), dma((16,)),
            dma((16,)), dma((16,)),
            dma((16,)), dma((16,)),
            dma((nf + nh + ns,)), dma((nf + nh + ns,)),
        ],
        name="back",
        compiler_params=pltpu.CompilerParams(
            collective_id=1, has_side_effects=True, vmem_limit_bytes=67043328
        ),
    )(q, k, v, dc, ctx, lse, ht, w, gm, frames, vec, gv, gc, ge, go)


def feed_kernel(
    ctx_ref, frames_ref, cot_ref, vec_ref, wo_ref, win_ref, wout_ref,
    fo_ref, gm_ref, dc_ref, gi_ref, gout_ref, go_ref, gv_ref,
    mid, h2, h2t, dyb, acc, dh2,
):
    b = pl.program_id(0)

    @pl.when(b == 0)
    def _():
        middle = frames_ref[...] + nn(ctx_ref[...].astype(BF), wo_ref[...]) + vec_ref[4:5, :]
        mid[...] = middle
        normed, _ = normalize(middle)
        hidden = (normed * vec_ref[5:6, :] + vec_ref[6:7, :]).astype(BF)
        h2[...] = hidden
        h2t[...] = hidden.T
        dyb[...] = cot_ref[...].astype(BF)
        acc[...] = middle + vec_ref[7:8, :]
        dh2[...] = jnp.zeros_like(dh2)
        gv_ref[...] = jnp.zeros_like(gv_ref)

    up = dyb[...]
    u = nn(h2[...], win_ref[...]) + vec_ref[pl.ds(8 + b, 1), :]
    phi = 0.5 * (1.0 + lax.erf(u * 0.7071067811865476))
    activated = (u * phi).astype(BF)
    acc[...] += nn(activated, wout_ref[...])
    gout_ref[...] = tn(activated, up).astype(BF)
    du = nt(up, wout_ref[...]) * (phi + u * jnp.exp(-0.5 * u * u) * 0.3989422804014327)
    gv_ref[pl.ds(8 + b, 1), :] = jnp.sum(du, axis=0, keepdims=True)
    dub = du.astype(BF)
    gi_ref[...] = nn(h2t[...], dub).astype(BF)
    dh2[...] += nt(dub, win_ref[...])

    @pl.when(b == pl.num_programs(0) - 1)
    def _():
        fo_ref[...] = acc[...]
        normed, inverse = normalize(mid[...])
        back, gain, offset = norm_back(dh2[...], normed, inverse, vec_ref[5:6, :])
        upstream = cot_ref[...]
        middle = upstream + back
        gm_ref[...] = middle
        dab = middle.astype(BF)
        go_ref[...] = tn(ctx_ref[...].astype(BF), dab).astype(BF)
        dctx = nt(dab, wo_ref[...]).astype(BF)
        dc_ref[...] = dctx
        gv_ref[3:4, :] = jnp.sum(dctx.astype(F32), axis=0, keepdims=True)
        gv_ref[4:5, :] = jnp.sum(middle, axis=0, keepdims=True)
        gv_ref[5:6, :] = gain[None]
        gv_ref[6:7, :] = offset[None]
        gv_ref[7:8, :] = jnp.sum(upstream, axis=0, keepdims=True)


def feed_all(ctx, frames, cot, vec, aw, ew, cw):
    rows, width = frames.shape
    full = ew.shape[1]
    whole = lambda shape: pl.BlockSpec(shape, lambda b: (0,) * len(shape))
    blocks = full // width
    return pl.pallas_call(
        feed_kernel,
        grid=(blocks,),
        out_shape=(
            jax.ShapeDtypeStruct((rows, width), F32),
            jax.ShapeDtypeStruct((rows, width), F32),
            jax.ShapeDtypeStruct((rows, width), BF),
            jax.ShapeDtypeStruct((width, full), BF),
            jax.ShapeDtypeStruct((full, width), BF),
            jax.ShapeDtypeStruct((width, width), BF),
            jax.ShapeDtypeStruct((16, width), F32),
        ),
        in_specs=[
            whole((rows, width)), whole((rows, width)), whole((rows, width)), whole((16, width)),
            pl.BlockSpec((None, width, width), lambda b: (3, 0, 0)),
            pl.BlockSpec((width, width), lambda b: (0, b)),
            pl.BlockSpec((width, width), lambda b: (b, 0)),
        ],
        out_specs=(
            whole((rows, width)), whole((rows, width)), whole((rows, width)),
            pl.BlockSpec((width, width), lambda b: (0, b)),
            pl.BlockSpec((width, width), lambda b: (b, 0)),
            whole((width, width)), whole((16, width)),
        ),
        scratch_shapes=[
            pltpu.VMEM((rows, width), F32),
            pltpu.VMEM((rows, width), BF),
            pltpu.VMEM((width, rows), BF),
            pltpu.VMEM((rows, width), BF),
            pltpu.VMEM((rows, width), F32),
            pltpu.VMEM((rows, width), F32),
        ],
        name="feed",
        compiler_params=pltpu.CompilerParams(vmem_limit_bytes=67043328),
    )(ctx, frames, cot, vec, aw, ew, cw)


def on_device(
    sizes,
    frames_in,
    cotangent,
    attention_weight,
    expand_weight,
    contract_weight,
    vectors,
    first_attention,
    first_expand,
    first_contract,
    first_vectors,
    second_attention,
    second_expand,
    second_contract,
    second_vectors,
):
    nd, nf, ns = sizes
    frames = frames_in[0]
    upstream = cotangent[0]
    rows, width = frames.shape
    shard = attention_weight.shape[1]
    full = expand_weight.shape[1]
    aw, ew, cw, vec, h_turned, queries, key_rows, value_rows, context_wide, log_total = front_all(
        sizes, frames, vectors, attention_weight, expand_weight, contract_weight
    )
    frames_out, grad_middle, grad_context, grad_expand, grad_contract, grad_output_w, gv = feed_all(
        context_wide, frames, upstream, vec, aw, ew, cw
    )
    oc, oe, oa, input_gradient, gv_sum = back_all(
        sizes,
        queries,
        key_rows,
        value_rows,
        grad_context,
        context_wide,
        log_total,
        h_turned,
        aw,
        grad_middle,
        frames,
        vec,
        gv,
        grad_contract.reshape(nf, 4, shard, width),
        grad_expand.reshape(nf, shard, full),
        grad_output_w.reshape(nf, shard, width),
    )
    owned_vec = lax.dynamic_slice_in_dim(
        gv_sum[:12], lax.axis_index("fsdp") * (width // nf), width // nf, 1
    )
    owned = (
        oa.reshape(4, shard, width).astype(F32),
        oe.astype(F32),
        oc.reshape(4 * shard, width).astype(F32),
    )
    attention_out = (owned[0],) + adam_update(
        attention_weight, owned[0], first_attention, second_attention, rate_matrix, decay_matrix
    )
    expand_out = (owned[1],) + adam_update(
        expand_weight, owned[1], first_expand, second_expand, rate_matrix, decay_matrix
    )
    contract_out = (owned[2],) + adam_update(
        contract_weight, owned[2], first_contract, second_contract, rate_matrix, decay_matrix
    )
    vector_out = (owned_vec,) + adam_update(
        vectors, owned_vec, first_vectors, second_vectors, rate_vector, 0.0
    )
    result = [frames_out[None], input_gradient[None]]
    for i in range(4):
        result += [attention_out[i], expand_out[i], contract_out[i], vector_out[i]]
    return tuple(result)


def solution(mesh):
    sizes = (mesh.shape["dp"], mesh.shape["fsdp"], mesh.shape["seq"])
    data = P(("dp", "fsdp"), "seq", None)
    state = (P(None, "fsdp", None), P("fsdp", None), P("fsdp", None), P(None, "fsdp"))
    return jax.shard_map(
        functools.partial(on_device, sizes),
        mesh=mesh,
        in_specs=(data, data) + state * 3,
        out_specs=(data, data) + state * 4,
        check_vma=False,
    )
```

profile of v0, /device:TPU:0, one launch (start us, length us, event | category | flops | bytes accessed | tf_op | source)
XLA Modules:
  0.0 289.4 jit_solution(16305706067888123887)
XLA Ops:
  0.7 79.9 %front.1 = (bf16[4,768,768]{2,1,0:T(8,128)(2,1)}, bf16[768,3072]{1,0:T(8,128)(2,1)}, bf16[3072,768]{1,0:T(8,128)(2,1)}, f32[16,768]{1,0:T(8,128)}, bf16[768,1536...) custom-call(f32[384,768]{1,0:T(8,128)} %bitcast.20, ...), custom_call_target="tpu_custom_call" | custom-call | tf_op jit(solution)/shard_map/front/pallas_call | solution.py:417
  80.6 23.7 %feed.1 = (f32[384,768]{1,0:T(8,128)}, f32[384,768]{1,0:T(8,128)}, bf16[384,768]{1,0:T(8,128)(2,1)}, bf16[768,3072]{1,0:T(8,128)(2,1)}, bf16[3072,768]{1,0:T(8,1...) custom-call(f32[384,768]{1,0:T(8,128)} %get-tuple-element.40.ctx_ref, f32[384,768]{1,0:T(8,128)} %bitcast.21, ...), custom_call_target="tpu_custom_call" | custom-call | tf_op jit(solution)/shard_map/feed/pallas_call | solution.py:1135
  104.3 148.2 %back.1 = (bf16[2,2,384,768]{3,2,1,0:T(8,128)(2,1)}, bf16[384,3072]{1,0:T(8,128)(2,1)}, bf16[2,2,384,768]{3,2,1,0:T(8,128)(2,1)}, f32[384,768]{1,0:T(8,128)}, f32[16,768]{1,0:T(8,128)}) custom-call(bf16[384,768]{1,0:T(8,128)(2,1)} %get-tuple-element.46.q_ref, bf16[1536,768]{1,0:T(8,128)(2,1)} %get-tuple-element.47.k_ref, ...), custom_call_target="tpu_custom_call" | custom-call | tf_op jit(solution)/shard_map/back/pallas_call | solution.py:1028
  252.5 0.0 copy-start.1
  252.5 0.0 slice-start
  252.5 0.0 slice-start.2
  252.5 0.0 slice-start.4
  252.6 13.7 %multiply_subtract_fusion.2 = (f32[4,384,768]{2,1,0:T(8,128)}, f32[4,384,768]{2,1,0:T(8,128)}, f32[4,384,768]{2,1,0:T(8,128)}, f32[4,384,768]{2,1,0:T(8,128)}) fusion(f32[4,384,768]{2,1,0:T(8,128)} %aw_ref.1, f32[4,384,768]{2,1,0:T(8,128)} %param.20, f32[4,384,768]{2,1,0:T(8,128)} %param.24, bf16[2,2,384,768]{3,2,1,0:T(8,128)(2,1)} %get-tuple-element.58), kind=kLoop, calls=%fused_computation.10 | loop fusion | flops 18874368 | bytes 35389440 | tf_op jit(solution)/shard_map/sub | solution.py:63
  266.2 0.0 copy-done.1
  266.2 0.0 slice-start.1
  266.2 0.0 slice-start.3
  266.2 0.0 slice-start.5
  266.3 0.0 copy-start
  266.3 13.2 %multiply_subtract_fusion.1 = (f32[384,3072]{1,0:T(8,128)}, f32[384,3072]{1,0:T(8,128)}, f32[384,3072]{1,0:T(8,128)}, f32[384,3072]{1,0:T(8,128)}) fusion(f32[384,3072]{1,0:T(8,128)} %ew_ref.1, f32[384,3072]{1,0:T(8,128)} %param.21, f32[384,3072]{1,0:T(8,128)} %param.25, bf16[384,3072]{1,0:T(8,128)(2,1)S(1)} %copy-done.1), kind=kLoop, calls=%fused_computation.8 | loop fusion | flops 18874368 | bytes 35389440 | tf_op jit(solution)/shard_map/sub | solution.py:63
  279.5 0.0 slice-done
  279.5 0.0 slice-done.2
  279.5 0.0 slice-done.4
  279.5 0.0 slice-done.1
  279.5 0.0 slice-done.3
  279.5 0.0 slice-done.5
  279.5 0.0 copy-done
  279.6 0.0 copy-start.3
  279.6 0.0 copy-start.4
  279.6 0.0 copy-start.5
  279.6 0.0 copy-start.6
  279.6 0.0 copy-start.2
  279.6 8.1 %multiply_subtract_fusion = (f32[1536,768]{1,0:T(8,128)}, f32[1536,768]{1,0:T(8,128)}, f32[1536,768]{1,0:T(8,128)}, f32[1536,768]{1,0:T(8,128)}) fusion(f32[1536,768]{1,0:T(8,128)S(1)} %bitcast.19, f32[1536,768]{1,0:T(8,128)S(1)} %bitcast.24, f32[1536,768]{1,0:T(8,128)S(1)} %bitcast.26, bf16[2,2,384,768]{3,2,1,0:T(8,128)(2,1)S(1)} %copy-done), kind=kLoop, calls=%fused_computation.6 | loop fusion | flops 18874368 | bytes 35389440 | tf_op jit(solution)/shard_map/sub | solution.py:63
  287.8 0.0 copy-done.3
  287.8 0.0 copy-done.4
  287.8 0.0 copy-done.5
  287.8 0.0 copy-done.6
  287.8 0.6 multiply_subtract_fusion.3
  288.4 0.0 copy-done.2
  288.4 1.0 copy.33
  (3 shorter events, 0.0 us)
Async XLA Ops:
  252.5 13.7 %copy-start.1 = (bf16[384,3072]{1,0:T(8,128)(2,1)S(1)}, bf16[384,3072]{1,0:T(8,128)(2,1)}, u32[]{:S(2)}) copy-start(bf16[384,3072]{1,0:T(8,128)(2,1)} %get-tuple-element.59) | copy-start | bytes 7077892
  252.5 27.0 %slice-start = ((s8[4718592]{0:T(1024)(128)(4,1)}), s8[4194304]{0:T(1024)(128)(4,1)S(1)}, s32[]{:S(2)}) async-start(s8[4718592]{0:T(1024)(128)(4,1)} %bitcast.18), calls=%async_computation | async-start | bytes 8388608
  252.5 27.0 %slice-start.2 = ((s8[4718592]{0:T(1024)(128)(4,1)}), s8[4194304]{0:T(1024)(128)(4,1)S(1)}, s32[]{:S(2)}) async-start(s8[4718592]{0:T(1024)(128)(4,1)} %bitcast.23), calls=%async_computation.2 | async-start | bytes 8388608
  252.5 27.0 %slice-start.4 = ((s8[4718592]{0:T(1024)(128)(4,1)}), s8[4194304]{0:T(1024)(128)(4,1)S(1)}, s32[]{:S(2)}) async-start(s8[4718592]{0:T(1024)(128)(4,1)} %bitcast.25), calls=%async_computation.4 | async-start | bytes 8388608
  266.2 13.3 %slice-start.1 = ((s8[4718592]{0:T(1024)(128)(4,1)}), s8[524288]{0:T(1024)(128)(4,1)S(1)}, s32[]{:S(2)}) async-start(s8[4718592]{0:T(1024)(128)(4,1)} %bitcast.18), calls=%async_computation.1 | async-start | bytes 1048576
  266.2 13.3 %slice-start.3 = ((s8[4718592]{0:T(1024)(128)(4,1)}), s8[524288]{0:T(1024)(128)(4,1)S(1)}, s32[]{:S(2)}) async-start(s8[4718592]{0:T(1024)(128)(4,1)} %bitcast.23), calls=%async_computation.3 | async-start | bytes 1048576
  266.2 13.3 %slice-start.5 = ((s8[4718592]{0:T(1024)(128)(4,1)}), s8[524288]{0:T(1024)(128)(4,1)S(1)}, s32[]{:S(2)}) async-start(s8[4718592]{0:T(1024)(128)(4,1)} %bitcast.25), calls=%async_computation.5 | async-start | bytes 1048576
  266.3 13.3 %copy-start = (bf16[2,2,384,768]{3,2,1,0:T(8,128)(2,1)S(1)}, bf16[2,2,384,768]{3,2,1,0:T(8,128)(2,1)}, u32[]{:S(2)}) copy-start(bf16[2,2,384,768]{3,2,1,0:T(8,128)(2,1)} %get-tuple-element.60) | copy-start | bytes 7077892
  279.6 8.2 %copy-start.3 = (f32[12,384]{1,0:T(8,128)S(1)}, f32[12,384]{1,0:T(8,128)}, u32[]{:S(2)}) copy-start(f32[12,384]{1,0:T(8,128)} %vec_ref.1) | copy-start | bytes 55300
  279.6 8.2 %copy-start.4 = (f32[12,384]{1,0:T(8,128)S(1)}, f32[12,384]{1,0:T(8,128)}, u32[]{:S(2)}) copy-start(f32[12,384]{1,0:T(8,128)} %param.23) | copy-start | bytes 55300
  279.6 8.2 %copy-start.5 = (f32[12,384]{1,0:T(8,128)S(1)}, f32[12,384]{1,0:T(8,128)}, u32[]{:S(2)}) copy-start(f32[12,384]{1,0:T(8,128)} %param.27) | copy-start | bytes 55300
  279.6 8.2 %copy-start.6 = (f32[16,768]{1,0:T(8,128)S(1)}, f32[16,768]{1,0:T(8,128)}, u32[]{:S(2)}) copy-start(f32[16,768]{1,0:T(8,128)} %get-tuple-element.61) | copy-start | bytes 147460
  279.6 8.8 %copy-start.2 = (f32[384,768]{1,0:T(8,128)S(1)}, f32[384,768]{1,0:T(8,128)}, u32[]{:S(2)}) copy-start(f32[384,768]{1,0:T(8,128)} %get-tuple-element.57) | copy-start | bytes 3538948
where the time goes:
time: 290 us; the launch traced here: 289 us
  Pallas kernels  252 us (87%)
  other arithmetic  35.7 us (12%)
    pallas_call x1, Pallas kernels, back_all(): pl.pallas_call(functools.partial(back_kernel, sizes), out_shape=(jax.Shap...  148 us
    pallas_call x1, Pallas kernels, front_all(): pl.pallas_call(functools.partial(front_kernel, sizes), out_shape=(jax.Sha...  79.9 us
    sub x4, other arithmetic, adam_update(): weight - rate * (first_hat / (jnp.sqrt(second_hat) + adam_eps) + decay *...  35.7 us
    pallas_call x1, Pallas kernels, feed_all(): pl.pallas_call(feed_kernel, grid=(blocks,), out_shape=(jax.ShapeDtypeStru...  23.7 us

commit v1 on v0

--- a/solution.py
+++ b/solution.py
@@ -148,24 +148,27 @@
         copy.start()
         vec_copies.append(copy)
 
+    order = (1, 2, 0, 3)
+
     def view(chunk, j, hi, core, own=False):
-        if chunk < 2:
-            first, count = ((0, 3), (3, 1))[chunk]
-            cols = width // nh
+        cols = width // nh
+        if chunk < 4:
             return a_ref.at[
-                pl.ds(first, count),
+                order[chunk],
                 pl.ds(pl.multiple_of(j * shard + core * half, 16), half),
                 pl.ds(pl.multiple_of(hi * cols, 128), cols),
             ]
-        ref, stage, size = ((e_ref, eb, shard), (c_ref, cb, deep))[chunk - 2]
-        cols = ref.shape[1] // nh
-        start = core * (size // 2)
-        if own:
-            ref = stage
-        else:
-            start = j * size + start
-        return ref.at[
-            pl.ds(pl.multiple_of(start, 16), size // 2),
+        if chunk < 8:
+            start = 0 if own else j * shard
+            wide = eb.shape[1] // nh
+            return (eb if own else e_ref).at[
+                pl.ds(pl.multiple_of(start + core * half, 16), half),
+                pl.ds(pl.multiple_of(hi * wide + (chunk - 4) * (wide // 4), 128), wide // 4),
+            ]
+        start = 0 if own else j * deep
+        tall = deep // 8
+        return (cb if own else c_ref).at[
+            pl.ds(pl.multiple_of(start + core * (deep // 2) + (chunk - 8) * tall, 16), tall),
             pl.ds(pl.multiple_of(hi * cols, 128), cols),
         ]
 
@@ -176,15 +179,15 @@
         for k in range(1, nf):
             copy = remote(
                 view(chunk, at.x, at.hi, at.core, True), view(chunk, at.x, at.hi, at.core),
-                xs.at[chunk, k], xr.at[chunk, k], at.x_peer(k),
+                xs.at[chunk, k - 1], xr.at[chunk, k - 1], at.x_peer(k),
             )
             copy.start()
             x_copies[chunk, k] = copy
 
     loads[0].wait()
-    for u in range(3):
+    for i, u in enumerate(order[:3]):
         a_ref[u, pl.ds(own, shard), :] = af[u].astype(BF)
-    send_chunk(0)
+        send_chunk(i)
     normed, _ = normalize(frames_ref[...])
     for copy in vec_copies:
         copy.wait()
@@ -214,14 +217,16 @@
     loads[1].wait()
     a_ref[3, pl.ds(own, shard), :] = af[3].astype(BF)
     loads[3].start()
-    send_chunk(1)
+    send_chunk(3)
     loads[2].wait()
     eb[...] = ef[...].astype(BF)
-    send_chunk(2)
+    for i in range(4, 8):
+        send_chunk(i)
     loads[3].wait()
     for u in range(4):
         cb[pl.ds(u * shard, shard), :] = af[u].astype(BF)
-    send_chunk(3)
+    for i in range(8, 12):
+        send_chunk(i)
     stores = [
         load(4, eb, e_ref.at[pl.ds(own, shard), :]),
         load(5, cb, c_ref.at[pl.ds(pl.multiple_of(at.x * deep, 16), deep), :]),
@@ -233,17 +238,17 @@
     def first_copy(chunk, k):
         j = lax.rem(at.x - k + nf, nf)
         piece = view(chunk, j, at.hi, at.core)
-        return remote(piece, piece, s1s.at[chunk, k], s1r.at[chunk, k], at.sibling())
+        return remote(piece, piece, s1s.at[chunk, k - 1], s1r.at[chunk, k - 1], at.sibling())
 
     def y_copy(chunk, k, m):
         j = lax.rem(at.x - k + nf, nf)
         piece = view(chunk, j, at.hi, at.core)
-        return remote(piece, piece, ys.at[chunk, k, m], yr.at[chunk, k, m], at.y_peer(m))
+        return remote(piece, piece, ys.at[chunk, k - 1, m - 1], yr.at[chunk, k - 1, m - 1], at.y_peer(m))
 
     def second_copy(chunk, k, m):
         j = lax.rem(at.x - k + nf, nf)
         piece = view(chunk, j, lax.rem(at.hi - m + nh, nh), at.core)
-        return remote(piece, piece, s2s.at[chunk, k, m], s2r.at[chunk, k, m], at.sibling())
+        return remote(piece, piece, s2s.at[chunk, k - 1, m - 1], s2r.at[chunk, k - 1, m - 1], at.sibling())
 
     def forward(chunk):
         for k in range(1, nf):
@@ -309,7 +314,13 @@
     assert ns == 4
     blocks = (at.z, at.z + 1 - 2 * b0, 2 - b1, 3 - 3 * b1)
 
-    def begin(i):
+    def tick(i):
+        if i < 12:
+            forward(i)
+        if i > 0:
+            relay(i - 1)
+
+    def begin(i, ticks):
         b = blocks[i]
         rows_of(b)
 
@@ -322,36 +333,40 @@
             stat[i, p] = jnp.where(
                 lo, jnp.where(lane < 32, found[0], found[1]), jnp.where(lane < 96, found[2], found[3])
             )
+            for when, which in ticks:
+                @pl.when(p == when)
+                def _(which=which):
+                    tick(which)
+
             return carry
 
         lax.fori_loop(0, width // 128, pair, 0)
 
-    forward(0)
+    tick(0)
+    tick(1)
+    tick(2)
     hop(1)
-    forward(1)
-    relay(0)
-    arrived(0)
+    tick(3)
+    for i in range(3):
+        arrived(i)
     q_buf[...] = (nn(h_ref[mine, :], a_ref[0]) + vec[2:3]).astype(BF)
     stores.append(load(6, q_buf, q_out))
     stores[-1].start()
-    begin(0)
+    tick(4)
+    begin(0, ((2, 5), (5, 6)))
     hop(2)
-    begin(1)
+    begin(1, ((1, 7), (4, 8)))
     turn(blocks[1])
-    relay(1)
-    forward(2)
-    begin(2)
+    begin(2, ((0, 9), (3, 10)))
     turn(blocks[2])
     hop(3)
     rows_of(blocks[3])
     turn(blocks[3])
-    arrived(1)
+    tick(11)
+    arrived(3)
     for i, (src, dst) in enumerate(((a_ref, a_out), (ht, ht_out), (k_buf, k_out), (v_buf2, v_out))):
         stores.append(load(7 + i, src, dst))
         stores[-1].start()
-    forward(3)
-    relay(2)
-
     def pair(p, carry):
         col = pl.ds(pl.multiple_of(p * 128, 128), 128)
         ctx, lse = [], []
@@ -376,20 +391,20 @@
 
         @pl.when(p == 1)
         def _():
-            relay(3)
+            tick(12)
 
         return carry
 
     lax.fori_loop(0, width // 128, pair, 0)
     stores.append(load(11, ctx_buf, ctx_out))
     stores[-1].start()
-    arrived(2)
-    arrived(3)
+    for i in range(4, 12):
+        arrived(i)
     for copy in stores:
         copy.wait()
     for copy in x_copies.values():
         copy.wait_send()
-    for chunk in range(4):
+    for chunk in range(12):
         for k in range(1, nf):
             first_copy(chunk, k).wait_send()
             for m in range(1, nh):
@@ -446,10 +461,10 @@
             pltpu.VMEM((ns - 1, width // 64, rows, rows), F32),
             pltpu.VMEM((ns - 1, width // 128, rows, 128), F32),
             dma((12,)),
-            dma((4, nf)), dma((4, nf)),
-            dma((4, nf, nh)), dma((4, nf, nh)),
-            dma((4, nf)), dma((4, nf)),
-            dma((4, nf, nh)), dma((4, nf, nh)),
+            dma((12, nf - 1)), dma((12, nf - 1)),
+            dma((12, nf - 1, nh - 1)), dma((12, nf - 1, nh - 1)),
+            dma((12, nf - 1)), dma((12, nf - 1)),
+            dma((12, nf - 1, nh - 1)), dma((12, nf - 1, nh - 1)),
             dma((nf,)), dma((nf,)),
             dma((ns,)), dma((ns,)), dma((ns,)),
         ],

time: 290 us -> 279 us (0.962)
  Pallas kernels: 252 us -> 242 us
    pallas_call x1, Pallas kernels: 79.9 us -> 69.8 us  [front_all(): pl.pallas_call(functools.partial(front_kernel, sizes), out_shape=(jax.Sha...]
where the time goes in v1:
time: 279 us
  Pallas kernels  242 us (87%)
  other arithmetic  35.7 us (13%)
    pallas_call x1, Pallas kernels, back_all(): pl.pallas_call(functools.partial(back_kernel, sizes), out_shape=(jax.Shap...  148 us
    pallas_call x1, Pallas kernels, front_all(): pl.pallas_call(functools.partial(front_kernel, sizes), out_shape=(jax.Sha...  69.8 us
    sub x4, other arithmetic, adam_update(): weight - rate * (first_hat / (jnp.sqrt(second_hat) + adam_eps) + decay *...  35.7 us
    pallas_call x1, Pallas kernels, feed_all(): pl.pallas_call(feed_kernel, grid=(blocks,), out_shape=(jax.ShapeDtypeStru...  23.7 us

profile of v1, /device:TPU:0, one launch (start us, length us, event | category | flops | bytes accessed | tf_op | source)
XLA Modules:
  0.0 279.2 jit_solution(532432279171028861)
XLA Ops:
  0.7 69.8 %front.1 = (bf16[4,768,768]{2,1,0:T(8,128)(2,1)}, bf16[768,3072]{1,0:T(8,128)(2,1)}, bf16[3072,768]{1,0:T(8,128)(2,1)}, f32[16,768]{1,0:T(8,128)}, bf16[768,1536...) custom-call(f32[384,768]{1,0:T(8,128)} %bitcast.20, ...), custom_call_target="tpu_custom_call" | custom-call | tf_op jit(solution)/shard_map/front/pallas_call | solution.py:432
  70.5 23.7 %feed.1 = (f32[384,768]{1,0:T(8,128)}, f32[384,768]{1,0:T(8,128)}, bf16[384,768]{1,0:T(8,128)(2,1)}, bf16[768,3072]{1,0:T(8,128)(2,1)}, bf16[3072,768]{1,0:T(8,1...) custom-call(f32[384,768]{1,0:T(8,128)} %get-tuple-element.40.ctx_ref, f32[384,768]{1,0:T(8,128)} %bitcast.21, ...), custom_call_target="tpu_custom_call" | custom-call | tf_op jit(solution)/shard_map/feed/pallas_call | solution.py:1150
  94.2 148.0 %back.1 = (bf16[2,2,384,768]{3,2,1,0:T(8,128)(2,1)}, bf16[384,3072]{1,0:T(8,128)(2,1)}, bf16[2,2,384,768]{3,2,1,0:T(8,128)(2,1)}, f32[384,768]{1,0:T(8,128)}, f32[16,768]{1,0:T(8,128)}) custom-call(bf16[384,768]{1,0:T(8,128)(2,1)} %get-tuple-element.46.q_ref, bf16[1536,768]{1,0:T(8,128)(2,1)} %get-tuple-element.47.k_ref, ...), custom_call_target="tpu_custom_call" | custom-call | tf_op jit(solution)/shard_map/back/pallas_call | solution.py:1043
  242.2 0.0 copy-start.1
  242.2 0.0 slice-start
  242.2 0.0 slice-start.2
  242.3 0.0 slice-start.4
  242.3 13.7 %multiply_subtract_fusion.2 = (f32[4,384,768]{2,1,0:T(8,128)}, f32[4,384,768]{2,1,0:T(8,128)}, f32[4,384,768]{2,1,0:T(8,128)}, f32[4,384,768]{2,1,0:T(8,128)}) fusion(f32[4,384,768]{2,1,0:T(8,128)} %aw_ref.1, f32[4,384,768]{2,1,0:T(8,128)} %param.20, f32[4,384,768]{2,1,0:T(8,128)} %param.24, bf16[2,2,384,768]{3,2,1,0:T(8,128)(2,1)} %get-tuple-element.58), kind=kLoop, calls=%fused_computation.10 | loop fusion | flops 18874368 | bytes 35389440 | tf_op jit(solution)/shard_map/sub | solution.py:63
  255.9 0.0 copy-done.1
  255.9 0.0 slice-start.1
  255.9 0.0 slice-start.3
  256.0 0.0 slice-start.5
  256.0 0.0 copy-start
  256.0 13.2 %multiply_subtract_fusion.1 = (f32[384,3072]{1,0:T(8,128)}, f32[384,3072]{1,0:T(8,128)}, f32[384,3072]{1,0:T(8,128)}, f32[384,3072]{1,0:T(8,128)}) fusion(f32[384,3072]{1,0:T(8,128)} %ew_ref.1, f32[384,3072]{1,0:T(8,128)} %param.21, f32[384,3072]{1,0:T(8,128)} %param.25, bf16[384,3072]{1,0:T(8,128)(2,1)S(1)} %copy-done.1), kind=kLoop, calls=%fused_computation.8 | loop fusion | flops 18874368 | bytes 35389440 | tf_op jit(solution)/shard_map/sub | solution.py:63
  269.2 0.0 slice-done
  269.2 0.0 slice-done.2
  269.2 0.0 slice-done.4
  269.2 0.0 slice-done.1
  269.2 0.0 slice-done.3
  269.2 0.0 slice-done.5
  269.2 0.0 copy-done
  269.3 0.0 copy-start.3
  269.3 0.0 copy-start.4
  269.3 0.0 copy-start.5
  269.3 0.0 copy-start.6
  269.3 0.0 copy-start.2
  269.3 8.1 %multiply_subtract_fusion = (f32[1536,768]{1,0:T(8,128)}, f32[1536,768]{1,0:T(8,128)}, f32[1536,768]{1,0:T(8,128)}, f32[1536,768]{1,0:T(8,128)}) fusion(f32[1536,768]{1,0:T(8,128)S(1)} %bitcast.19, f32[1536,768]{1,0:T(8,128)S(1)} %bitcast.24, f32[1536,768]{1,0:T(8,128)S(1)} %bitcast.26, bf16[2,2,384,768]{3,2,1,0:T(8,128)(2,1)S(1)} %copy-done), kind=kLoop, calls=%fused_computation.6 | loop fusion | flops 18874368 | bytes 35389440 | tf_op jit(solution)/shard_map/sub | solution.py:63
  277.5 0.0 copy-done.3
  277.5 0.0 copy-done.4
  277.5 0.0 copy-done.5
  277.5 0.0 copy-done.6
  277.5 0.6 multiply_subtract_fusion.3
  278.1 0.0 copy-done.2
  278.1 1.0 copy.33
  (3 shorter events, 0.0 us)
Async XLA Ops:
  242.2 13.7 %copy-start.1 = (bf16[384,3072]{1,0:T(8,128)(2,1)S(1)}, bf16[384,3072]{1,0:T(8,128)(2,1)}, u32[]{:S(2)}) copy-start(bf16[384,3072]{1,0:T(8,128)(2,1)} %get-tuple-element.59) | copy-start | bytes 7077892
  242.2 27.0 %slice-start = ((s8[4718592]{0:T(1024)(128)(4,1)}), s8[4194304]{0:T(1024)(128)(4,1)S(1)}, s32[]{:S(2)}) async-start(s8[4718592]{0:T(1024)(128)(4,1)} %bitcast.18), calls=%async_computation | async-start | bytes 8388608
  242.2 27.0 %slice-start.2 = ((s8[4718592]{0:T(1024)(128)(4,1)}), s8[4194304]{0:T(1024)(128)(4,1)S(1)}, s32[]{:S(2)}) async-start(s8[4718592]{0:T(1024)(128)(4,1)} %bitcast.23), calls=%async_computation.2 | async-start | bytes 8388608
  242.3 27.0 %slice-start.4 = ((s8[4718592]{0:T(1024)(128)(4,1)}), s8[4194304]{0:T(1024)(128)(4,1)S(1)}, s32[]{:S(2)}) async-start(s8[4718592]{0:T(1024)(128)(4,1)} %bitcast.25), calls=%async_computation.4 | async-start | bytes 8388608
  255.9 13.3 %slice-start.1 = ((s8[4718592]{0:T(1024)(128)(4,1)}), s8[524288]{0:T(1024)(128)(4,1)S(1)}, s32[]{:S(2)}) async-start(s8[4718592]{0:T(1024)(128)(4,1)} %bitcast.18), calls=%async_computation.1 | async-start | bytes 1048576
  255.9 13.3 %slice-start.3 = ((s8[4718592]{0:T(1024)(128)(4,1)}), s8[524288]{0:T(1024)(128)(4,1)S(1)}, s32[]{:S(2)}) async-start(s8[4718592]{0:T(1024)(128)(4,1)} %bitcast.23), calls=%async_computation.3 | async-start | bytes 1048576
  256.0 13.3 %slice-start.5 = ((s8[4718592]{0:T(1024)(128)(4,1)}), s8[524288]{0:T(1024)(128)(4,1)S(1)}, s32[]{:S(2)}) async-start(s8[4718592]{0:T(1024)(128)(4,1)} %bitcast.25), calls=%async_computation.5 | async-start | bytes 1048576
  256.0 13.3 %copy-start = (bf16[2,2,384,768]{3,2,1,0:T(8,128)(2,1)S(1)}, bf16[2,2,384,768]{3,2,1,0:T(8,128)(2,1)}, u32[]{:S(2)}) copy-start(bf16[2,2,384,768]{3,2,1,0:T(8,128)(2,1)} %get-tuple-element.60) | copy-start | bytes 7077892
  269.3 8.2 %copy-start.3 = (f32[12,384]{1,0:T(8,128)S(1)}, f32[12,384]{1,0:T(8,128)}, u32[]{:S(2)}) copy-start(f32[12,384]{1,0:T(8,128)} %vec_ref.1) | copy-start | bytes 55300
  269.3 8.2 %copy-start.4 = (f32[12,384]{1,0:T(8,128)S(1)}, f32[12,384]{1,0:T(8,128)}, u32[]{:S(2)}) copy-start(f32[12,384]{1,0:T(8,128)} %param.23) | copy-start | bytes 55300
  269.3 8.2 %copy-start.5 = (f32[12,384]{1,0:T(8,128)S(1)}, f32[12,384]{1,0:T(8,128)}, u32[]{:S(2)}) copy-start(f32[12,384]{1,0:T(8,128)} %param.27) | copy-start | bytes 55300
  269.3 8.2 %copy-start.6 = (f32[16,768]{1,0:T(8,128)S(1)}, f32[16,768]{1,0:T(8,128)}, u32[]{:S(2)}) copy-start(f32[16,768]{1,0:T(8,128)} %get-tuple-element.61) | copy-start | bytes 147460
  269.3 8.8 %copy-start.2 = (f32[384,768]{1,0:T(8,128)S(1)}, f32[384,768]{1,0:T(8,128)}, u32[]{:S(2)}) copy-start(f32[384,768]{1,0:T(8,128)} %get-tuple-element.57) | copy-start | bytes 3538948

commit v2 on v1

--- a/solution.py
+++ b/solution.py
@@ -481,7 +481,7 @@
     oc_ref, oe_ref, oa_ref, ig_ref, ov_ref,
     ga, own, rc, rx, ry, rz, ri, dkt, dvt, dqa, dhs, dra, drb, drc, vb, vx, vy, vz,
     os, cs, cr, xs, xr, ys, yr, zs, zr, zis, zir, gs, gr, ays, ayr, acs, acr,
-    das, dar, dbs, dbr, dcs, dcr, vs, vr,
+    das, dar, dbs, dbr, dcs, dcr, dns, dnr, vs, vr,
 ):
     at = Place(sizes)
     nf, nh, ns = at.nf, at.nh, at.ns
@@ -781,7 +781,7 @@
 
     pieces = 16
     per_step = 2
-    lag = 2
+    lag = 1
     low = 1 - b1
 
     def part_of(t):
@@ -789,8 +789,16 @@
 
     def da_copy(t):
         return remote(
-            dhs.at[pl.ds(low, 3), part_of(t)], dra.at[:, part_of(t)], das.at[t], dar.at[t], near
+            dhs.at[pl.ds(2 * low, 2), part_of(t)], dra.at[:, part_of(t)], das.at[t], dar.at[t], near
         )
+
+    def dn_start(t):
+        remote(
+            dhs.at[at.z + 1 - 2 * b0, part_of(t)], drc.at[part_of(t)], dns.at[0], dnr.at[0], near
+        ).start()
+
+    def dn_whole():
+        return remote(dhs.at[0], drc, dns.at[0], dnr.at[0], near)
 
     def db_copy(t):
         return remote(
@@ -810,8 +818,8 @@
             @pl.when(inner)
             def _():
                 da_copy(t).wait_recv()
-                for j in range(3):
-                    dhs[low + j, part] = dhs[low + j, part] + dra[j, part]
+                for j in range(2):
+                    dhs[2 * low + j, part] = dhs[2 * low + j, part] + dra[j, part]
                 db_copy(t).start()
         elif i == 2:
             @pl.when(inner)
@@ -834,7 +842,7 @@
     def first_norm():
         @pl.when(inner)
         def _():
-            drc[...] = jnp.zeros_like(drc)
+            dn_whole().wait_recv()
 
         total = dhs[at.z].astype(F32) + nt(w_ref[0], dqa[...].astype(BF))
         total += drc[...].astype(F32)
@@ -903,8 +911,11 @@
     ready = group
     each = -(-2 * pairs // ready)
     done = [-(-pairs * (i + 1) // each) - 1 for i in range(2)]
-    away = done[1] + 1
-    norm = max(away + (pieces - 1) // per_step + 4, chunks - 2)
+    away = done[0] + 1
+    slack = 2
+    turns = pieces // per_step
+    rest = away + turns
+    norm = max(away + turns + 3 * slack, rest + turns // 2 + 1, chunks - 2)
     stages = (stage_x, stage_y, stage_z, stage_zi, stage_g, stage_ay)
     last = max(chunks + lag * len(stages), norm + 6)
     for n in range(4):
@@ -961,12 +972,17 @@
                 stage(n - lag * i)
 
         for i in range(4):
-            first = away + i
-
-            @pl.when(jnp.logical_and(n >= first, n < first + pieces // per_step))
+            first = away + slack * i
+
+            @pl.when(jnp.logical_and(n >= first, n < first + turns))
             def _(i=i, first=first):
                 for t in range(per_step):
                     d_stage(i, (n - first) * per_step + t)
+
+        @pl.when(jnp.logical_and(outer, jnp.logical_and(n >= rest, n < rest + turns // 2)))
+        def _():
+            for t in range(2 * per_step):
+                dn_start((n - rest) * (2 * per_step) + t)
 
         for i in range(5):
             @pl.when(n == norm + i)
@@ -1002,6 +1018,8 @@
 
     @pl.when(outer)
     def _():
+        dn_whole().wait_send()
+
         def sent(t, carry):
             da_copy(t).wait_send()
             return carry
@@ -1063,7 +1081,7 @@
             pltpu.VMEM((width, every), BF),
             pltpu.VMEM((rows, width), F32),
             pltpu.VMEM((ns, width, rows), BF),
-            pltpu.VMEM((3, width, rows), BF),
+            pltpu.VMEM((2, width, rows), BF),
             pltpu.VMEM((2, width, rows), BF),
             pltpu.VMEM((width, rows), BF),
             pltpu.VMEM((3, 16, width), F32),
@@ -1082,6 +1100,7 @@
             dma((16,)), dma((16,)),
             dma((16,)), dma((16,)),
             dma((16,)), dma((16,)),
+            dma((1,)), dma((1,)),
             dma((nf + nh + ns,)), dma((nf + nh + ns,)),
         ],
         name="back",

time: 279 us -> 265 us (0.950)
  Pallas kernels: 242 us -> 227 us
    pallas_call x1, Pallas kernels: 148 us -> 134 us  [back_all(): pl.pallas_call(functools.partial(back_kernel, sizes), out_shape=(jax.Shap...]
where the time goes in v2:
time: 265 us
  Pallas kernels  227 us (86%)
  other arithmetic  35.7 us (13%)
    pallas_call x1, Pallas kernels, back_all(): pl.pallas_call(functools.partial(back_kernel, sizes), out_shape=(jax.Shap...  134 us
    pallas_call x1, Pallas kernels, front_all(): pl.pallas_call(functools.partial(front_kernel, sizes), out_shape=(jax.Sha...  69.8 us
    sub x4, other arithmetic, adam_update(): weight - rate * (first_hat / (jnp.sqrt(second_hat) + adam_eps) + decay *...  35.7 us
    pallas_call x1, Pallas kernels, feed_all(): pl.pallas_call(feed_kernel, grid=(blocks,), out_shape=(jax.ShapeDtypeStru...  23.7 us

profile of v2, /device:TPU:0, one launch (start us, length us, event | category | flops | bytes accessed | tf_op | source)
XLA Modules:
  0.0 264.9 jit_solution(9072120131450808189)
XLA Ops:
  0.7 69.8 %front.1 = (bf16[4,768,768]{2,1,0:T(8,128)(2,1)}, bf16[768,3072]{1,0:T(8,128)(2,1)}, bf16[3072,768]{1,0:T(8,128)(2,1)}, f32[16,768]{1,0:T(8,128)}, bf16[768,1536...) custom-call(f32[384,768]{1,0:T(8,128)} %bitcast.20, ...), custom_call_target="tpu_custom_call" | custom-call | tf_op jit(solution)/shard_map/front/pallas_call | solution.py:432
  70.5 23.7 %feed.1 = (f32[384,768]{1,0:T(8,128)}, f32[384,768]{1,0:T(8,128)}, bf16[384,768]{1,0:T(8,128)(2,1)}, bf16[768,3072]{1,0:T(8,128)(2,1)}, bf16[3072,768]{1,0:T(8,1...) custom-call(f32[384,768]{1,0:T(8,128)} %get-tuple-element.40.ctx_ref, f32[384,768]{1,0:T(8,128)} %bitcast.21, ...), custom_call_target="tpu_custom_call" | custom-call | tf_op jit(solution)/shard_map/feed/pallas_call | solution.py:1169
  94.2 133.7 %back.1 = (bf16[2,2,384,768]{3,2,1,0:T(8,128)(2,1)}, bf16[384,3072]{1,0:T(8,128)(2,1)}, bf16[2,2,384,768]{3,2,1,0:T(8,128)(2,1)}, f32[384,768]{1,0:T(8,128)}, f32[16,768]{1,0:T(8,128)}) custom-call(bf16[384,768]{1,0:T(8,128)(2,1)} %get-tuple-element.46.q_ref, bf16[1536,768]{1,0:T(8,128)(2,1)} %get-tuple-element.47.k_ref, ...), custom_call_target="tpu_custom_call" | custom-call | tf_op jit(solution)/shard_map/back/pallas_call | solution.py:1061
  227.9 0.0 copy-start.1
  227.9 0.0 slice-start
  227.9 0.0 slice-start.2
  228.0 0.0 slice-start.4
  228.0 13.7 %multiply_subtract_fusion.2 = (f32[4,384,768]{2,1,0:T(8,128)}, f32[4,384,768]{2,1,0:T(8,128)}, f32[4,384,768]{2,1,0:T(8,128)}, f32[4,384,768]{2,1,0:T(8,128)}) fusion(f32[4,384,768]{2,1,0:T(8,128)} %aw_ref.1, f32[4,384,768]{2,1,0:T(8,128)} %param.20, f32[4,384,768]{2,1,0:T(8,128)} %param.24, bf16[2,2,384,768]{3,2,1,0:T(8,128)(2,1)} %get-tuple-element.58), kind=kLoop, calls=%fused_computation.10 | loop fusion | flops 18874368 | bytes 35389440 | tf_op jit(solution)/shard_map/sub | solution.py:63
  241.6 0.0 copy-done.1
  241.6 0.0 slice-start.1
  241.7 0.0 slice-start.3
  241.7 0.0 slice-start.5
  241.7 0.0 copy-start
  241.7 13.2 %multiply_subtract_fusion.1 = (f32[384,3072]{1,0:T(8,128)}, f32[384,3072]{1,0:T(8,128)}, f32[384,3072]{1,0:T(8,128)}, f32[384,3072]{1,0:T(8,128)}) fusion(f32[384,3072]{1,0:T(8,128)} %ew_ref.1, f32[384,3072]{1,0:T(8,128)} %param.21, f32[384,3072]{1,0:T(8,128)} %param.25, bf16[384,3072]{1,0:T(8,128)(2,1)S(1)} %copy-done.1), kind=kLoop, calls=%fused_computation.8 | loop fusion | flops 18874368 | bytes 35389440 | tf_op jit(solution)/shard_map/sub | solution.py:63
  254.9 0.0 slice-done
  254.9 0.0 slice-done.2
  254.9 0.0 slice-done.4
  254.9 0.0 slice-done.1
  254.9 0.0 slice-done.3
  254.9 0.0 slice-done.5
  255.0 0.0 copy-done
  255.0 0.0 copy-start.3
  255.0 0.0 copy-start.4
  255.0 0.0 copy-start.5
  255.0 0.0 copy-start.6
  255.0 0.0 copy-start.2
  255.0 8.1 %multiply_subtract_fusion = (f32[1536,768]{1,0:T(8,128)}, f32[1536,768]{1,0:T(8,128)}, f32[1536,768]{1,0:T(8,128)}, f32[1536,768]{1,0:T(8,128)}) fusion(f32[1536,768]{1,0:T(8,128)S(1)} %bitcast.19, f32[1536,768]{1,0:T(8,128)S(1)} %bitcast.24, f32[1536,768]{1,0:T(8,128)S(1)} %bitcast.26, bf16[2,2,384,768]{3,2,1,0:T(8,128)(2,1)S(1)} %copy-done), kind=kLoop, calls=%fused_computation.6 | loop fusion | flops 18874368 | bytes 35389440 | tf_op jit(solution)/shard_map/sub | solution.py:63
  263.2 0.0 copy-done.3
  263.2 0.0 copy-done.4
  263.2 0.0 copy-done.5
  263.2 0.0 copy-done.6
  263.2 0.6 multiply_subtract_fusion.3
  263.9 0.0 copy-done.2
  263.9 1.0 copy.33
  (3 shorter events, 0.0 us)
Async XLA Ops:
  227.9 13.7 %copy-start.1 = (bf16[384,3072]{1,0:T(8,128)(2,1)S(1)}, bf16[384,3072]{1,0:T(8,128)(2,1)}, u32[]{:S(2)}) copy-start(bf16[384,3072]{1,0:T(8,128)(2,1)} %get-tuple-element.59) | copy-start | bytes 7077892
  227.9 27.0 %slice-start = ((s8[4718592]{0:T(1024)(128)(4,1)}), s8[4194304]{0:T(1024)(128)(4,1)S(1)}, s32[]{:S(2)}) async-start(s8[4718592]{0:T(1024)(128)(4,1)} %bitcast.18), calls=%async_computation | async-start | bytes 8388608
  227.9 27.0 %slice-start.2 = ((s8[4718592]{0:T(1024)(128)(4,1)}), s8[4194304]{0:T(1024)(128)(4,1)S(1)}, s32[]{:S(2)}) async-start(s8[4718592]{0:T(1024)(128)(4,1)} %bitcast.23), calls=%async_computation.2 | async-start | bytes 8388608
  228.0 27.0 %slice-start.4 = ((s8[4718592]{0:T(1024)(128)(4,1)}), s8[4194304]{0:T(1024)(128)(4,1)S(1)}, s32[]{:S(2)}) async-start(s8[4718592]{0:T(1024)(128)(4,1)} %bitcast.25), calls=%async_computation.4 | async-start | bytes 8388608
  241.6 13.3 %slice-start.1 = ((s8[4718592]{0:T(1024)(128)(4,1)}), s8[524288]{0:T(1024)(128)(4,1)S(1)}, s32[]{:S(2)}) async-start(s8[4718592]{0:T(1024)(128)(4,1)} %bitcast.18), calls=%async_computation.1 | async-start | bytes 1048576
  241.7 13.3 %slice-start.3 = ((s8[4718592]{0:T(1024)(128)(4,1)}), s8[524288]{0:T(1024)(128)(4,1)S(1)}, s32[]{:S(2)}) async-start(s8[4718592]{0:T(1024)(128)(4,1)} %bitcast.23), calls=%async_computation.3 | async-start | bytes 1048576
  241.7 13.3 %slice-start.5 = ((s8[4718592]{0:T(1024)(128)(4,1)}), s8[524288]{0:T(1024)(128)(4,1)S(1)}, s32[]{:S(2)}) async-start(s8[4718592]{0:T(1024)(128)(4,1)} %bitcast.25), calls=%async_computation.5 | async-start | bytes 1048576
  241.7 13.3 %copy-start = (bf16[2,2,384,768]{3,2,1,0:T(8,128)(2,1)S(1)}, bf16[2,2,384,768]{3,2,1,0:T(8,128)(2,1)}, u32[]{:S(2)}) copy-start(bf16[2,2,384,768]{3,2,1,0:T(8,128)(2,1)} %get-tuple-element.60) | copy-start | bytes 7077892
  255.0 8.2 %copy-start.3 = (f32[12,384]{1,0:T(8,128)S(1)}, f32[12,384]{1,0:T(8,128)}, u32[]{:S(2)}) copy-start(f32[12,384]{1,0:T(8,128)} %vec_ref.1) | copy-start | bytes 55300
  255.0 8.2 %copy-start.4 = (f32[12,384]{1,0:T(8,128)S(1)}, f32[12,384]{1,0:T(8,128)}, u32[]{:S(2)}) copy-start(f32[12,384]{1,0:T(8,128)} %param.23) | copy-start | bytes 55300
  255.0 8.2 %copy-start.5 = (f32[12,384]{1,0:T(8,128)S(1)}, f32[12,384]{1,0:T(8,128)}, u32[]{:S(2)}) copy-start(f32[12,384]{1,0:T(8,128)} %param.27) | copy-start | bytes 55300
  255.0 8.2 %copy-start.6 = (f32[16,768]{1,0:T(8,128)S(1)}, f32[16,768]{1,0:T(8,128)}, u32[]{:S(2)}) copy-start(f32[16,768]{1,0:T(8,128)} %get-tuple-element.61) | copy-start | bytes 147460
  255.0 8.8 %copy-start.2 = (f32[384,768]{1,0:T(8,128)S(1)}, f32[384,768]{1,0:T(8,128)}, u32[]{:S(2)}) copy-start(f32[384,768]{1,0:T(8,128)} %get-tuple-element.57) | copy-start | bytes 3538948

commit v3 on v2

--- a/solution.py
+++ b/solution.py
@@ -781,7 +781,7 @@
 
     pieces = 16
     per_step = 2
-    lag = 1
+    offsets = (0, 1, 3, 4, 5, 7)
     low = 1 - b1
 
     def part_of(t):
@@ -908,28 +908,34 @@
                 total += vz[j]
             ov_ref[...] = total
 
-    ready = group
+    ready = 8 if split == 2 else group
     each = -(-2 * pairs // ready)
-    done = [-(-pairs * (i + 1) // each) - 1 for i in range(2)]
+
+    def units_before(n):
+        return (2 * pairs * n + ready - 1) // ready
+
+    done = [
+        next(n for n in range(ready) if units_before(n + 1) >= pairs * (i + 1)) for i in range(2)
+    ]
     away = done[0] + 1
     slack = 2
     turns = pieces // per_step
     rest = away + turns
     norm = max(away + turns + 3 * slack, rest + turns // 2 + 1, chunks - 2)
     stages = (stage_x, stage_y, stage_z, stage_zi, stage_g, stage_ay)
-    last = max(chunks + lag * len(stages), norm + 6)
+    last = max(chunks + offsets[-1] + 1, norm + 6)
     for n in range(4):
         c_send(n)
 
     def step(n, carry):
-        for k in range(2):
-            @pl.when(2 * n + k < 2 * group)
+        for k in range(3):
+            @pl.when(3 * n + k < 2 * group)
             def _(k=k):
-                stage_c(2 * n + k)
-
-                @pl.when(2 * n + k + 4 < 2 * group)
+                stage_c(3 * n + k)
+
+                @pl.when(3 * n + k + 4 < 2 * group)
                 def _():
-                    c_send(2 * n + k + 4)
+                    c_send(3 * n + k + 4)
 
         @pl.when(jnp.logical_and(n >= ready + 1, n < ready + 1 + per))
         def _():
@@ -939,9 +945,9 @@
         @pl.when(n < ready)
         def _():
             def one(k, carry):
-                @pl.when(n * each + k < 2 * pairs)
+                @pl.when(units_before(n) + k < units_before(n + 1))
                 def _():
-                    unit(n * each + k)
+                    unit(units_before(n) + k)
 
                 return carry
 
@@ -967,9 +973,9 @@
                 c_send(2 * group + (n - ready) * split + r)
 
         for i, stage in enumerate(stages):
-            @pl.when(jnp.logical_and(n >= lag * i, n < chunks + lag * i))
+            @pl.when(jnp.logical_and(n >= offsets[i], n < chunks + offsets[i]))
             def _(i=i, stage=stage):
-                stage(n - lag * i)
+                stage(n - offsets[i])
 
         for i in range(4):
             first = away + slack * i

time: 265 us -> 260 us (0.981)
  Pallas kernels: 227 us -> 222 us
    pallas_call x1, Pallas kernels: 134 us -> 129 us  [back_all(): pl.pallas_call(functools.partial(back_kernel, sizes), out_shape=(jax.Shap...]
where the time goes in v3:
time: 260 us
  Pallas kernels  222 us (85%)
  other arithmetic  35.7 us (14%)
    pallas_call x1, Pallas kernels, back_all(): pl.pallas_call(functools.partial(back_kernel, sizes), out_shape=(jax.Shap...  129 us
    pallas_call x1, Pallas kernels, front_all(): pl.pallas_call(functools.partial(front_kernel, sizes), out_shape=(jax.Sha...  69.8 us
    sub x4, other arithmetic, adam_update(): weight - rate * (first_hat / (jnp.sqrt(second_hat) + adam_eps) + decay *...  35.7 us
    pallas_call x1, Pallas kernels, feed_all(): pl.pallas_call(feed_kernel, grid=(blocks,), out_shape=(jax.ShapeDtypeStru...  23.7 us

profile of v3, /device:TPU:0, one launch (start us, length us, event | category | flops | bytes accessed | tf_op | source)
XLA Modules:
  0.0 259.8 jit_solution(9925447342507424374)
XLA Ops:
  0.7 69.8 %front.1 = (bf16[4,768,768]{2,1,0:T(8,128)(2,1)}, bf16[768,3072]{1,0:T(8,128)(2,1)}, bf16[3072,768]{1,0:T(8,128)(2,1)}, f32[16,768]{1,0:T(8,128)}, bf16[768,1536...) custom-call(f32[384,768]{1,0:T(8,128)} %bitcast.20, ...), custom_call_target="tpu_custom_call" | custom-call | tf_op jit(solution)/shard_map/front/pallas_call | solution.py:432
  70.5 23.7 %feed.1 = (f32[384,768]{1,0:T(8,128)}, f32[384,768]{1,0:T(8,128)}, bf16[384,768]{1,0:T(8,128)(2,1)}, bf16[768,3072]{1,0:T(8,128)(2,1)}, bf16[3072,768]{1,0:T(8,1...) custom-call(f32[384,768]{1,0:T(8,128)} %get-tuple-element.40.ctx_ref, f32[384,768]{1,0:T(8,128)} %bitcast.21, ...), custom_call_target="tpu_custom_call" | custom-call | tf_op jit(solution)/shard_map/feed/pallas_call | solution.py:1175
  94.2 128.7 %back.1 = (bf16[2,2,384,768]{3,2,1,0:T(8,128)(2,1)}, bf16[384,3072]{1,0:T(8,128)(2,1)}, bf16[2,2,384,768]{3,2,1,0:T(8,128)(2,1)}, f32[384,768]{1,0:T(8,128)}, f32[16,768]{1,0:T(8,128)}) custom-call(bf16[384,768]{1,0:T(8,128)(2,1)} %get-tuple-element.46.q_ref, bf16[1536,768]{1,0:T(8,128)(2,1)} %get-tuple-element.47.k_ref, ...), custom_call_target="tpu_custom_call" | custom-call | tf_op jit(solution)/shard_map/back/pallas_call | solution.py:1067
  222.9 0.0 copy-start.1
  222.9 0.0 slice-start
  222.9 0.0 slice-start.2
  222.9 0.0 slice-start.4
  222.9 13.7 %multiply_subtract_fusion.2 = (f32[4,384,768]{2,1,0:T(8,128)}, f32[4,384,768]{2,1,0:T(8,128)}, f32[4,384,768]{2,1,0:T(8,128)}, f32[4,384,768]{2,1,0:T(8,128)}) fusion(f32[4,384,768]{2,1,0:T(8,128)} %aw_ref.1, f32[4,384,768]{2,1,0:T(8,128)} %param.20, f32[4,384,768]{2,1,0:T(8,128)} %param.24, bf16[2,2,384,768]{3,2,1,0:T(8,128)(2,1)} %get-tuple-element.58), kind=kLoop, calls=%fused_computation.10 | loop fusion | flops 18874368 | bytes 35389440 | tf_op jit(solution)/shard_map/sub | solution.py:63
  236.6 0.0 copy-done.1
  236.6 0.0 slice-start.1
  236.6 0.0 slice-start.3
  236.6 0.0 slice-start.5
  236.7 0.0 copy-start
  236.7 13.2 %multiply_subtract_fusion.1 = (f32[384,3072]{1,0:T(8,128)}, f32[384,3072]{1,0:T(8,128)}, f32[384,3072]{1,0:T(8,128)}, f32[384,3072]{1,0:T(8,128)}) fusion(f32[384,3072]{1,0:T(8,128)} %ew_ref.1, f32[384,3072]{1,0:T(8,128)} %param.21, f32[384,3072]{1,0:T(8,128)} %param.25, bf16[384,3072]{1,0:T(8,128)(2,1)S(1)} %copy-done.1), kind=kLoop, calls=%fused_computation.8 | loop fusion | flops 18874368 | bytes 35389440 | tf_op jit(solution)/shard_map/sub | solution.py:63
  249.9 0.0 slice-done
  249.9 0.0 slice-done.2
  249.9 0.0 slice-done.4
  249.9 0.0 slice-done.1
  249.9 0.0 slice-done.3
  249.9 0.0 slice-done.5
  249.9 0.0 copy-done
  250.0 0.0 copy-start.3
  250.0 0.0 copy-start.4
  250.0 0.0 copy-start.5
  250.0 0.0 copy-start.6
  250.0 0.0 copy-start.2
  250.0 8.1 %multiply_subtract_fusion = (f32[1536,768]{1,0:T(8,128)}, f32[1536,768]{1,0:T(8,128)}, f32[1536,768]{1,0:T(8,128)}, f32[1536,768]{1,0:T(8,128)}) fusion(f32[1536,768]{1,0:T(8,128)S(1)} %bitcast.19, f32[1536,768]{1,0:T(8,128)S(1)} %bitcast.24, f32[1536,768]{1,0:T(8,128)S(1)} %bitcast.26, bf16[2,2,384,768]{3,2,1,0:T(8,128)(2,1)S(1)} %copy-done), kind=kLoop, calls=%fused_computation.6 | loop fusion | flops 18874368 | bytes 35389440 | tf_op jit(solution)/shard_map/sub | solution.py:63
  258.1 0.0 copy-done.3
  258.2 0.0 copy-done.4
  258.2 0.0 copy-done.5
  258.2 0.0 copy-done.6
  258.2 0.6 multiply_subtract_fusion.3
  258.8 0.0 copy-done.2
  258.8 1.0 copy.33
  (3 shorter events, 0.0 us)
Async XLA Ops:
  222.9 13.7 %copy-start.1 = (bf16[384,3072]{1,0:T(8,128)(2,1)S(1)}, bf16[384,3072]{1,0:T(8,128)(2,1)}, u32[]{:S(2)}) copy-start(bf16[384,3072]{1,0:T(8,128)(2,1)} %get-tuple-element.59) | copy-start | bytes 7077892
  222.9 27.0 %slice-start = ((s8[4718592]{0:T(1024)(128)(4,1)}), s8[4194304]{0:T(1024)(128)(4,1)S(1)}, s32[]{:S(2)}) async-start(s8[4718592]{0:T(1024)(128)(4,1)} %bitcast.18), calls=%async_computation | async-start | bytes 8388608
  222.9 27.0 %slice-start.2 = ((s8[4718592]{0:T(1024)(128)(4,1)}), s8[4194304]{0:T(1024)(128)(4,1)S(1)}, s32[]{:S(2)}) async-start(s8[4718592]{0:T(1024)(128)(4,1)} %bitcast.23), calls=%async_computation.2 | async-start | bytes 8388608
  222.9 27.0 %slice-start.4 = ((s8[4718592]{0:T(1024)(128)(4,1)}), s8[4194304]{0:T(1024)(128)(4,1)S(1)}, s32[]{:S(2)}) async-start(s8[4718592]{0:T(1024)(128)(4,1)} %bitcast.25), calls=%async_computation.4 | async-start | bytes 8388608
  236.6 13.3 %slice-start.1 = ((s8[4718592]{0:T(1024)(128)(4,1)}), s8[524288]{0:T(1024)(128)(4,1)S(1)}, s32[]{:S(2)}) async-start(s8[4718592]{0:T(1024)(128)(4,1)} %bitcast.18), calls=%async_computation.1 | async-start | bytes 1048576
  236.6 13.3 %slice-start.3 = ((s8[4718592]{0:T(1024)(128)(4,1)}), s8[524288]{0:T(1024)(128)(4,1)S(1)}, s32[]{:S(2)}) async-start(s8[4718592]{0:T(1024)(128)(4,1)} %bitcast.23), calls=%async_computation.3 | async-start | bytes 1048576
  236.6 13.3 %slice-start.5 = ((s8[4718592]{0:T(1024)(128)(4,1)}), s8[524288]{0:T(1024)(128)(4,1)S(1)}, s32[]{:S(2)}) async-start(s8[4718592]{0:T(1024)(128)(4,1)} %bitcast.25), calls=%async_computation.5 | async-start | bytes 1048576
  236.7 13.3 %copy-start = (bf16[2,2,384,768]{3,2,1,0:T(8,128)(2,1)S(1)}, bf16[2,2,384,768]{3,2,1,0:T(8,128)(2,1)}, u32[]{:S(2)}) copy-start(bf16[2,2,384,768]{3,2,1,0:T(8,128)(2,1)} %get-tuple-element.60) | copy-start | bytes 7077892
  250.0 8.2 %copy-start.3 = (f32[12,384]{1,0:T(8,128)S(1)}, f32[12,384]{1,0:T(8,128)}, u32[]{:S(2)}) copy-start(f32[12,384]{1,0:T(8,128)} %vec_ref.1) | copy-start | bytes 55300
  250.0 8.2 %copy-start.4 = (f32[12,384]{1,0:T(8,128)S(1)}, f32[12,384]{1,0:T(8,128)}, u32[]{:S(2)}) copy-start(f32[12,384]{1,0:T(8,128)} %param.23) | copy-start | bytes 55300
  250.0 8.2 %copy-start.5 = (f32[12,384]{1,0:T(8,128)S(1)}, f32[12,384]{1,0:T(8,128)}, u32[]{:S(2)}) copy-start(f32[12,384]{1,0:T(8,128)} %param.27) | copy-start | bytes 55300
  250.0 8.2 %copy-start.6 = (f32[16,768]{1,0:T(8,128)S(1)}, f32[16,768]{1,0:T(8,128)}, u32[]{:S(2)}) copy-start(f32[16,768]{1,0:T(8,128)} %get-tuple-element.61) | copy-start | bytes 147460
  250.0 8.8 %copy-start.2 = (f32[384,768]{1,0:T(8,128)S(1)}, f32[384,768]{1,0:T(8,128)}, u32[]{:S(2)}) copy-start(f32[384,768]{1,0:T(8,128)} %get-tuple-element.57) | copy-start | bytes 3538948

commit v4 on v3

--- a/solution.py
+++ b/solution.py
@@ -781,7 +781,7 @@
 
     pieces = 16
     per_step = 2
-    offsets = (0, 1, 3, 4, 5, 7)
+    offsets = (0, 1, 3, 4, 5, 6)
     low = 1 - b1
 
     def part_of(t):
@@ -1119,7 +1119,7 @@
 def feed_kernel(
     ctx_ref, frames_ref, cot_ref, vec_ref, wo_ref, win_ref, wout_ref,
     fo_ref, gm_ref, dc_ref, gi_ref, gout_ref, go_ref, gv_ref,
-    mid, h2, h2t, dyb, acc, dh2,
+    mid, h2, h2t, dyb, acc, dh2, act, dub,
 ):
     b = pl.program_id(0)
 
@@ -1136,17 +1136,24 @@
         dh2[...] = jnp.zeros_like(dh2)
         gv_ref[...] = jnp.zeros_like(gv_ref)
 
-    up = dyb[...]
-    u = nn(h2[...], win_ref[...]) + vec_ref[pl.ds(8 + b, 1), :]
-    phi = 0.5 * (1.0 + lax.erf(u * 0.7071067811865476))
-    activated = (u * phi).astype(BF)
-    acc[...] += nn(activated, wout_ref[...])
-    gout_ref[...] = tn(activated, up).astype(BF)
-    du = nt(up, wout_ref[...]) * (phi + u * jnp.exp(-0.5 * u * u) * 0.3989422804014327)
-    gv_ref[pl.ds(8 + b, 1), :] = jnp.sum(du, axis=0, keepdims=True)
-    dub = du.astype(BF)
-    gi_ref[...] = nn(h2t[...], dub).astype(BF)
-    dh2[...] += nt(dub, win_ref[...])
+    bias = vec_ref[pl.ds(8 + b, 1), :]
+    size = h2.shape[0] // 1
+    total = None
+    for i in range(1):
+        part = pl.ds(i * size, size)
+        u = nn(h2[part, :], win_ref[...]) + bias
+        da = nt(dyb[part, :], wout_ref[...])
+        phi = 0.5 * (1.0 + lax.erf(u * 0.7071067811865476))
+        act[part, :] = (u * phi).astype(BF)
+        du = da * (phi + u * jnp.exp(-0.5 * u * u) * 0.3989422804014327)
+        found = jnp.sum(du, axis=0, keepdims=True)
+        total = found if total is None else total + found
+        dub[part, :] = du.astype(BF)
+    gv_ref[pl.ds(8 + b, 1), :] = total
+    acc[...] += nn(act[...], wout_ref[...])
+    gout_ref[...] = tn(act[...], dyb[...]).astype(BF)
+    gi_ref[...] = nn(h2t[...], dub[...]).astype(BF)
+    dh2[...] += nt(dub[...], win_ref[...])
 
     @pl.when(b == pl.num_programs(0) - 1)
     def _():
@@ -1203,6 +1210,8 @@
             pltpu.VMEM((rows, width), BF),
             pltpu.VMEM((rows, width), F32),
             pltpu.VMEM((rows, width), F32),
+            pltpu.VMEM((rows, width), BF),
+            pltpu.VMEM((rows, width), BF),
         ],
         name="feed",
         compiler_params=pltpu.CompilerParams(vmem_limit_bytes=67043328),

time: 260 us -> 259 us (level)
  no operation moved by 1% of the time
where the time goes in v4:
time: 259 us
  Pallas kernels  221 us (85%)
  other arithmetic  35.7 us (14%)
    pallas_call x1, Pallas kernels, back_all(): pl.pallas_call(functools.partial(back_kernel, sizes), out_shape=(jax.Shap...  128 us
    pallas_call x1, Pallas kernels, front_all(): pl.pallas_call(functools.partial(front_kernel, sizes), out_shape=(jax.Sha...  69.8 us
    sub x4, other arithmetic, adam_update(): weight - rate * (first_hat / (jnp.sqrt(second_hat) + adam_eps) + decay *...  35.7 us
    pallas_call x1, Pallas kernels, feed_all(): pl.pallas_call(feed_kernel, grid=(blocks,), out_shape=(jax.ShapeDtypeStru...  23 us

profile of v4, /device:TPU:0, one launch (start us, length us, event | category | flops | bytes accessed | tf_op | source)
XLA Modules:
  0.0 258.9 jit_solution(239495603260009412)
XLA Ops:
  0.7 69.8 %front.1 = (bf16[4,768,768]{2,1,0:T(8,128)(2,1)}, bf16[768,3072]{1,0:T(8,128)(2,1)}, bf16[3072,768]{1,0:T(8,128)(2,1)}, f32[16,768]{1,0:T(8,128)}, bf16[768,1536...) custom-call(f32[384,768]{1,0:T(8,128)} %bitcast.20, ...), custom_call_target="tpu_custom_call" | custom-call | tf_op jit(solution)/shard_map/front/pallas_call | solution.py:432
  70.5 23.0 %feed.1 = (f32[384,768]{1,0:T(8,128)}, f32[384,768]{1,0:T(8,128)}, bf16[384,768]{1,0:T(8,128)(2,1)}, bf16[768,3072]{1,0:T(8,128)(2,1)}, bf16[3072,768]{1,0:T(8,1...) custom-call(f32[384,768]{1,0:T(8,128)} %get-tuple-element.40.ctx_ref, f32[384,768]{1,0:T(8,128)} %bitcast.21, ...), custom_call_target="tpu_custom_call" | custom-call | tf_op jit(solution)/shard_map/feed/pallas_call | solution.py:1182
  93.5 128.4 %back.1 = (bf16[2,2,384,768]{3,2,1,0:T(8,128)(2,1)}, bf16[384,3072]{1,0:T(8,128)(2,1)}, bf16[2,2,384,768]{3,2,1,0:T(8,128)(2,1)}, f32[384,768]{1,0:T(8,128)}, f32[16,768]{1,0:T(8,128)}) custom-call(bf16[384,768]{1,0:T(8,128)(2,1)} %get-tuple-element.46.q_ref, bf16[1536,768]{1,0:T(8,128)(2,1)} %get-tuple-element.47.k_ref, ...), custom_call_target="tpu_custom_call" | custom-call | tf_op jit(solution)/shard_map/back/pallas_call | solution.py:1067
  221.9 0.0 copy-start.1
  221.9 0.0 slice-start
  221.9 0.0 slice-start.2
  221.9 0.0 slice-start.4
  222.0 13.7 %multiply_subtract_fusion.2 = (f32[4,384,768]{2,1,0:T(8,128)}, f32[4,384,768]{2,1,0:T(8,128)}, f32[4,384,768]{2,1,0:T(8,128)}, f32[4,384,768]{2,1,0:T(8,128)}) fusion(f32[4,384,768]{2,1,0:T(8,128)} %aw_ref.1, f32[4,384,768]{2,1,0:T(8,128)} %param.20, f32[4,384,768]{2,1,0:T(8,128)} %param.24, bf16[2,2,384,768]{3,2,1,0:T(8,128)(2,1)} %get-tuple-element.58), kind=kLoop, calls=%fused_computation.10 | loop fusion | flops 18874368 | bytes 35389440 | tf_op jit(solution)/shard_map/sub | solution.py:63
  235.6 0.0 copy-done.1
  235.6 0.0 slice-start.1
  235.6 0.0 slice-start.3
  235.7 0.0 slice-start.5
  235.7 0.0 copy-start
  235.7 13.2 %multiply_subtract_fusion.1 = (f32[384,3072]{1,0:T(8,128)}, f32[384,3072]{1,0:T(8,128)}, f32[384,3072]{1,0:T(8,128)}, f32[384,3072]{1,0:T(8,128)}) fusion(f32[384,3072]{1,0:T(8,128)} %ew_ref.1, f32[384,3072]{1,0:T(8,128)} %param.21, f32[384,3072]{1,0:T(8,128)} %param.25, bf16[384,3072]{1,0:T(8,128)(2,1)S(1)} %copy-done.1), kind=kLoop, calls=%fused_computation.8 | loop fusion | flops 18874368 | bytes 35389440 | tf_op jit(solution)/shard_map/sub | solution.py:63
  248.9 0.0 slice-done
  248.9 0.0 slice-done.2
  248.9 0.0 slice-done.4
  248.9 0.0 slice-done.1
  248.9 0.0 slice-done.3
  248.9 0.0 slice-done.5
  248.9 0.0 copy-done
  249.0 0.0 copy-start.3
  249.0 0.0 copy-start.4
  249.0 0.0 copy-start.5
  249.0 0.0 copy-start.6
  249.0 0.0 copy-start.2
  249.0 8.1 %multiply_subtract_fusion = (f32[1536,768]{1,0:T(8,128)}, f32[1536,768]{1,0:T(8,128)}, f32[1536,768]{1,0:T(8,128)}, f32[1536,768]{1,0:T(8,128)}) fusion(f32[1536,768]{1,0:T(8,128)S(1)} %bitcast.19, f32[1536,768]{1,0:T(8,128)S(1)} %bitcast.24, f32[1536,768]{1,0:T(8,128)S(1)} %bitcast.26, bf16[2,2,384,768]{3,2,1,0:T(8,128)(2,1)S(1)} %copy-done), kind=kLoop, calls=%fused_computation.6 | loop fusion | flops 18874368 | bytes 35389440 | tf_op jit(solution)/shard_map/sub | solution.py:63
  257.2 0.0 copy-done.3
  257.2 0.0 copy-done.4
  257.2 0.0 copy-done.5
  257.2 0.0 copy-done.6
  257.2 0.6 multiply_subtract_fusion.3
  257.8 0.0 copy-done.2
  257.8 1.0 copy.33
  (3 shorter events, 0.0 us)
Async XLA Ops:
  221.9 13.7 %copy-start.1 = (bf16[384,3072]{1,0:T(8,128)(2,1)S(1)}, bf16[384,3072]{1,0:T(8,128)(2,1)}, u32[]{:S(2)}) copy-start(bf16[384,3072]{1,0:T(8,128)(2,1)} %get-tuple-element.59) | copy-start | bytes 7077892
  221.9 27.0 %slice-start = ((s8[4718592]{0:T(1024)(128)(4,1)}), s8[4194304]{0:T(1024)(128)(4,1)S(1)}, s32[]{:S(2)}) async-start(s8[4718592]{0:T(1024)(128)(4,1)} %bitcast.18), calls=%async_computation | async-start | bytes 8388608
  221.9 27.0 %slice-start.2 = ((s8[4718592]{0:T(1024)(128)(4,1)}), s8[4194304]{0:T(1024)(128)(4,1)S(1)}, s32[]{:S(2)}) async-start(s8[4718592]{0:T(1024)(128)(4,1)} %bitcast.23), calls=%async_computation.2 | async-start | bytes 8388608
  221.9 27.0 %slice-start.4 = ((s8[4718592]{0:T(1024)(128)(4,1)}), s8[4194304]{0:T(1024)(128)(4,1)S(1)}, s32[]{:S(2)}) async-start(s8[4718592]{0:T(1024)(128)(4,1)} %bitcast.25), calls=%async_computation.4 | async-start | bytes 8388608
  235.6 13.3 %slice-start.1 = ((s8[4718592]{0:T(1024)(128)(4,1)}), s8[524288]{0:T(1024)(128)(4,1)S(1)}, s32[]{:S(2)}) async-start(s8[4718592]{0:T(1024)(128)(4,1)} %bitcast.18), calls=%async_computation.1 | async-start | bytes 1048576
  235.6 13.3 %slice-start.3 = ((s8[4718592]{0:T(1024)(128)(4,1)}), s8[524288]{0:T(1024)(128)(4,1)S(1)}, s32[]{:S(2)}) async-start(s8[4718592]{0:T(1024)(128)(4,1)} %bitcast.23), calls=%async_computation.3 | async-start | bytes 1048576
  235.7 13.3 %slice-start.5 = ((s8[4718592]{0:T(1024)(128)(4,1)}), s8[524288]{0:T(1024)(128)(4,1)S(1)}, s32[]{:S(2)}) async-start(s8[4718592]{0:T(1024)(128)(4,1)} %bitcast.25), calls=%async_computation.5 | async-start | bytes 1048576
  235.7 13.3 %copy-start = (bf16[2,2,384,768]{3,2,1,0:T(8,128)(2,1)S(1)}, bf16[2,2,384,768]{3,2,1,0:T(8,128)(2,1)}, u32[]{:S(2)}) copy-start(bf16[2,2,384,768]{3,2,1,0:T(8,128)(2,1)} %get-tuple-element.60) | copy-start | bytes 7077892
  249.0 8.2 %copy-start.3 = (f32[12,384]{1,0:T(8,128)S(1)}, f32[12,384]{1,0:T(8,128)}, u32[]{:S(2)}) copy-start(f32[12,384]{1,0:T(8,128)} %vec_ref.1) | copy-start | bytes 55300
  249.0 8.2 %copy-start.4 = (f32[12,384]{1,0:T(8,128)S(1)}, f32[12,384]{1,0:T(8,128)}, u32[]{:S(2)}) copy-start(f32[12,384]{1,0:T(8,128)} %param.23) | copy-start | bytes 55300
  249.0 8.2 %copy-start.5 = (f32[12,384]{1,0:T(8,128)S(1)}, f32[12,384]{1,0:T(8,128)}, u32[]{:S(2)}) copy-start(f32[12,384]{1,0:T(8,128)} %param.27) | copy-start | bytes 55300
  249.0 8.2 %copy-start.6 = (f32[16,768]{1,0:T(8,128)S(1)}, f32[16,768]{1,0:T(8,128)}, u32[]{:S(2)}) copy-start(f32[16,768]{1,0:T(8,128)} %get-tuple-element.61) | copy-start | bytes 147460
  249.0 8.8 %copy-start.2 = (f32[384,768]{1,0:T(8,128)S(1)}, f32[384,768]{1,0:T(8,128)}, u32[]{:S(2)}) copy-start(f32[384,768]{1,0:T(8,128)} %get-tuple-element.57) | copy-start | bytes 3538948
